TPU v7x, 512 devices: a whole 4x8x8 slice. The times are simulated.
512 devices in a mesh: grp: 128 (over y, z, core), slab: 4 (over x).
Axes of the slice: x: 4, y: 8, z: 8, core: 2. Of those that a mesh axis runs over, the one named last changes fastest.
Arguments:
- grids: float32 [128, 512, 4096], P('grp', 'slab'), may hold values from -6 to 6
- first_level: int32 [128], P('grp'), may hold values from 6 to 8, as said below
- coeffs: int32 [128], P('grp'), may hold values from -3 to 3
- slot_map: int32 [128, 512], P('grp', 'slab'), may hold values from 0 to 1023, as said below
Outputs:
- combined_grid: float32 [128, 512, 4096], P('grp', 'slab')
Inputs may be any that keep to these rules, and one draw needn't show every extreme that they name: The second dimension of grid g has level 9 minus first_level[g]. Every value of the range is taken by some grid. `slot_map`: grid g's point with first coordinate i of 2^a points lies at position i / 2^a of a periodic unit interval, and likewise in the second dimension. Two rows of any grids at the same position in the first two dimensions share a slot; rows of one grid have distinct slots; every slot is used by some grid. The rows held by the s-th index of slab (first coordinates in the s-th of 4 equal ranges) of every grid have slots in the s-th of 4 equal aligned ranges of the 1024 slots.
All inputs are finite; a program needn't handle non-finite values.
Results may differ from a plain program's by a relative error of at most 0.0003.
Values sent between devices are 32-bit elements; how exact they have to be, the bound alone decides.
No kernel may reach another device: no remote copies, remote signals or barrier semaphores. Data moves between devices by JAX's collectives and lax.ppermute only.
A program may use at most 64 MiB of HBM per device.

v0:
```python
import functools

import jax
import jax.numpy as jnp
import numpy as np
from jax import lax
from jax.experimental import pallas as pl
from jax.experimental.pallas import tpu as pltpu
from jax.sharding import PartitionSpec as P

LEVEL_SUM = 9
LOW_LEVEL = 6
NY = 8
NZ = 8
MEMBERS = 4
ROWS = 128
PLANE = 8
BLOCK = 32
SLOTS = 7
THERE = SLOTS * BLOCK
FLAGS = THERE + PLANE
SENT = FLAGS + 8
ENTRY = 2 * (ROWS + PLANE)
TABLE = 8 * BLOCK + PLANE
LANES = 128


def slots_of(levels):
    six, seven, eight = (level in levels for level in (6, 7, 8))
    third = 3 if six else (5 if seven else None)
    fifth = 6 if eight else (5 if six and seven else None)
    return (0, 1, 2, third, 4, fifth, 7)


def place_of(x, y):
    if x % 4 == 0 and y % 4 == 0:
        return (x // 4) * 2 + y // 4
    if x % 4 == 0 and y % 2 == 0:
        return 32 + (x // 4) * 2 + y // 4
    if x % 4 == 2 and y % 4 == 0:
        return 64 + (x // 4) * 2 + y // 4
    if x % 4 == 0:
        return 96 + (x // 4) * 4 + y // 2
    if x % 4 == 2:
        return 160 + (x // 4) * 2 + y // 4
    return 192 + (x // 2) * 2 + y // 4


def hier_line(n):
    h = np.zeros((n, n), np.float32)
    for j in range(n):
        h[j, j] += 1.0
        if j:
            s = j & -j
            h[j, j - s] -= 0.5
            h[j, (j + s) % n] -= 0.5
    return h


def dehier_line(n):
    e = np.zeros((n, n), np.float32)
    e[:, 0] = 1.0
    for k in range(1, n):
        for j in range(n):
            d = min(abs(j - k), n - abs(j - k))
            e[j, k] = max(0.0, 1.0 - d / (k & -k))
    return e


def one_grid(level, slots):
    n = 1 << (LEVEL_SUM - level)
    span = ROWS // n
    hy, ey = hier_line(n), dehier_line(n)
    forth = np.zeros((SENT, ROWS + PLANE), np.float32)
    back = np.zeros((ROWS, FLAGS), np.float32)
    for i in range(span):
        for y in range(n):
            t = place_of(i * 64 // span, y * 8 // n)
            m = BLOCK * slots.index(t // BLOCK) + t % BLOCK
            s = i & -i
            steps = [(i, 1.0)] + ([(i - s, -0.5), (i + s, -0.5)] if i else [])
            for j, w in steps:
                forth[m, j * n : j * n + n] += w * hy[y]
            for j in range(span):
                w = max(0.0, 1.0 - abs(j - i) / s) if i else 1.0 - j / span
                back[j * n : j * n + n, m] += w * ey[:, y]
    for y in range(n):
        t = THERE + y * 8 // n
        forth[t, ROWS : ROWS + n] += hy[y]
        for j in range(span):
            back[j * n : j * n + n, t] += j / span * ey[:, y]
    return forth, back


@functools.cache
def row_tables():
    forth, back = [], []
    for own in (6, 7, 8):
        for other in (6, 7, 8):
            slots = slots_of((own, other))
            mine, theirs = one_grid(own, slots), one_grid(other, slots)
            forth.append(np.concatenate([mine[0], theirs[0]], axis=1))
            back.append(mine[1])
    return np.stack(forth), np.stack(back)


def two_part_dot(table, values):
    high = values.astype(jnp.bfloat16)
    low = (values - high.astype(jnp.float32)).astype(jnp.bfloat16)
    dot = functools.partial(jnp.dot, preferred_element_type=jnp.float32)
    return dot(table, high) + dot(table, low)


def number_in(ref, row):
    return jnp.max(ref[row : row + 1, :LANES])


def core_here():
    return lax.axis_index("grp") % 2


def piece_here(turn):
    me = lax.axis_index("grp")
    core, z, y = me % 2, me // 2 % NZ, me // (2 * NZ)
    return ((y + core) % 2 * 2 + (z + core) % 2) ^ turn


def half_of(ref, core, rows=slice(None)):
    width = ref.shape[1] // 2
    return ref.at[rows, pl.ds(pl.multiple_of(core * width, LANES), width)]


def entry_kernel(level_ref, coeff_ref, rows_ref, out_ref, own_ref, other_ref):
    core = core_here()
    half = out_ref.shape[1]
    mine = pl.ds(pl.multiple_of(core * half, LANES), half)
    theirs = pl.ds(pl.multiple_of((1 - core) * half, LANES), half)
    own_ref[...] = rows_ref[:PLANE, mine]
    other_ref[...] = rows_ref[:PLANE, theirs]
    out_ref[:ROWS, :] = rows_ref[:, theirs]
    line = lax.broadcasted_iota(jnp.int32, (8, half), 0)
    out_ref[ROWS:, :] = jnp.where(line == 0, level_ref[...], coeff_ref[...]).astype(jnp.float32)


def forth_kernel(level_ref, coeff_ref, table_ref, rows_ref, own_next_ref, other_ref, other_next_ref, *outs):
    *out_refs, meta_ref = outs
    own_level = level_ref[0]
    other_level = number_in(other_ref, ROWS).astype(jnp.int32)
    which = (own_level - LOW_LEVEL) * 3 + other_level - LOW_LEVEL
    chunk = out_refs[0].shape[1]
    lane = lax.broadcasted_iota(jnp.int32, (1, ENTRY), 1)
    scale = jnp.where(lane < ENTRY // 2, coeff_ref[0].astype(jnp.float32), number_in(other_ref, ROWS + 1))
    table = (table_ref[which].astype(jnp.float32) * scale).astype(jnp.bfloat16)
    six = jnp.logical_or(own_level == 6, other_level == 6).astype(jnp.float32)
    eight = jnp.logical_or(own_level == 8, other_level == 8).astype(jnp.float32)
    width = chunk // 2
    line = lax.broadcasted_iota(jnp.int32, (SENT - FLAGS, width), 0)
    flags = jnp.where(line == 0, six, eight)
    first = core_here() * MEMBERS * chunk
    for turn, out_ref in enumerate(out_refs):
        for h in range(2):
            here = slice(h * width, (h + 1) * width)
            low = piece_here(turn) * chunk + h * width
            span = pl.ds(pl.multiple_of(low, LANES), width)
            own = rows_ref[:, pl.ds(pl.multiple_of(first + low, LANES), width)]
            values = jnp.concatenate(
                [own, own_next_ref[:, span], other_ref[:ROWS, span], other_next_ref[:, span]], axis=0
            )
            out_ref[:, here] = two_part_dot(table, values)
            out_ref[FLAGS:SENT, here] = flags
    meta_ref[...] = other_ref[ROWS:, :LANES]


def add_kernel(*refs):
    *got_refs, out_ref = refs
    for j in range(MEMBERS):
        lanes = slice(j * LANES, (j + 1) * LANES)
        six = [ref[FLAGS : FLAGS + 1, lanes] == 1.0 for ref in got_refs]
        eight = [ref[FLAGS + 1 : FLAGS + 2, lanes] == 1.0 for ref in got_refs]
        slot = lambda k, i: got_refs[k][BLOCK * i : BLOCK * (i + 1), lanes]
        terms = (
            lambda k: slot(k, 0),
            lambda k: slot(k, 1),
            lambda k: slot(k, 2),
            lambda k: jnp.where(six[k], slot(k, 3), 0.0),
            lambda k: slot(k, 4),
            lambda k: jnp.where(six[k], jnp.where(eight[k], 0.0, slot(k, 5)), slot(k, 3)),
            lambda k: jnp.where(eight[k], slot(k, 5), 0.0),
            lambda k: slot(k, 6),
            lambda k: got_refs[k][THERE:FLAGS, lanes],
        )
        for block, term in enumerate(terms):
            total = term(0)
            for k in range(1, MEMBERS):
                total = total + term(k)
            out_ref[j, BLOCK * block : BLOCK * block + total.shape[0], :] = total


def total_kernel(got_ref, out_ref):
    total = got_ref[0]
    for k in range(1, MEMBERS):
        total = total + got_ref[k]
    for k in range(MEMBERS):
        out_ref[k] = total


def pick_kernel(table_ref, *refs):
    for got_ref, out_ref in zip(refs[:MEMBERS], refs[MEMBERS:]):
        for j in range(MEMBERS):
            lanes = slice(j * LANES, (j + 1) * LANES)
            block = lambda i: table_ref[j, BLOCK * i : BLOCK * (i + 1), :]
            six = got_ref[FLAGS : FLAGS + 1, lanes] == 1.0
            eight = got_ref[FLAGS + 1 : FLAGS + 2, lanes] == 1.0
            out_ref[0:32, lanes] = block(0)
            out_ref[32:64, lanes] = block(1)
            out_ref[64:96, lanes] = block(2)
            out_ref[96:128, lanes] = jnp.where(six, block(3), block(5))
            out_ref[128:160, lanes] = block(4)
            out_ref[160:192, lanes] = jnp.where(eight, block(6), block(5))
            out_ref[192:224, lanes] = block(7)
            out_ref[THERE:FLAGS, lanes] = table_ref[j, 8 * BLOCK : TABLE, :]


def levels_in(level_ref, meta_ref):
    return level_ref[0] - LOW_LEVEL, number_in(meta_ref, 0).astype(jnp.int32) - LOW_LEVEL


def pieces(refs):
    for turn, ref in enumerate(refs):
        chunk = ref.shape[1]
        for h in range(2):
            width = chunk // 2
            yield piece_here(turn) * chunk + h * width, ref[:, h * width : (h + 1) * width]


def other_back_kernel(level_ref, meta_ref, table_ref, *refs):
    *got_refs, out_ref = refs
    own, other = levels_in(level_ref, meta_ref)
    table = table_ref[other * 3 + own]
    for low, values in pieces(got_refs):
        out_ref[:, pl.ds(pl.multiple_of(low, LANES), values.shape[1])] = two_part_dot(table, values)


def own_back_kernel(level_ref, meta_ref, table_ref, *refs):
    *got_refs, out_ref, done_ref, sems = refs
    own, other = levels_in(level_ref, meta_ref)
    table = table_ref[own * 3 + other]
    first = core_here() * (out_ref.shape[1] // 2)
    copies = []
    for i, (low, values) in enumerate(pieces(got_refs)):
        width = values.shape[1]
        done_ref[i] = two_part_dot(table, values)
        start = pl.multiple_of(first + low, LANES)
        copy = pltpu.make_async_copy(done_ref.at[i], out_ref.at[:, pl.ds(start, width)], sems.at[i])
        copy.start()
        copies.append(copy)
    for copy in copies:
        copy.wait()


def place_kernel(values_ref, filled_ref, out_ref, sem):
    copy = pltpu.make_async_copy(values_ref, half_of(out_ref, 1 - core_here()), sem)
    copy.start()
    copy.wait()


def member(y, z, core):
    return (y % NY * NZ + z % NZ) * 2 + core


TILES = [
    [member(2 * a + i + core, 2 * b + j + core, core) for i in (0, 1) for j in (0, 1)]
    for core in (0, 1)
    for a in range(NY // 2)
    for b in range(NZ // 2)
]
ALONG_Y = [[[member(2 * a + i, z, core) for a in range(NY // 2)] for i in (0, 1) for z in range(NZ)] for core in (0, 1)]
ALONG_Z = [[[member(y, 2 * b + j, core) for b in range(NZ // 2)] for j in (0, 1) for y in range(NY)] for core in (0, 1)]
LINES = ALONG_Y[0] + ALONG_Z[1]
OTHER_LINES = ALONG_Z[0] + ALONG_Y[1]
VMEM = pl.BlockSpec(memory_space=pltpu.VMEM)
SMEM = pl.BlockSpec(memory_space=pltpu.SMEM)
HBM = pl.BlockSpec(memory_space=pltpu.HBM)
DMA = pltpu.SemaphoreType.DMA


def exchange(values, groups):
    return lax.all_to_all(values, "grp", 0, 0, axis_index_groups=groups, tiled=True)


def f32(*shape):
    return jax.ShapeDtypeStruct(shape, jnp.float32)


def call(kernel, ins, outs, shapes, scratch=(), limit=16, flops=0, moved=0, alias=None):
    return pl.pallas_call(
        kernel,
        in_specs=ins,
        out_specs=outs,
        out_shape=shapes,
        scratch_shapes=scratch,
        compiler_params=pltpu.CompilerParams(vmem_limit_bytes=limit << 20),
        cost_estimate=pl.CostEstimate(flops=flops, bytes_accessed=moved, transcendentals=0),
        input_output_aliases=alias or {},
    )


def shards(grids, first_level, coeffs, slot_map):
    rows = grids[0]
    width = rows.shape[1]
    half = width // 2
    chunk = half // MEMBERS
    slabs = lax.axis_size("slab")
    members = lax.axis_size("grp")
    swap = [(i, i ^ 1) for i in range(members)]
    forth, back = (jnp.asarray(table, jnp.bfloat16) for table in row_tables())

    def to_previous(values, turn):
        pairs = [
            (g * slabs + s, (g ^ turn) * slabs + (s - 1) % slabs)
            for g in range(members)
            for s in range(slabs)
        ]
        return lax.ppermute(values, ("grp", "slab"), pairs)

    def through_tile(pieces):
        turned = lambda turn: [(tile[i], tile[i ^ turn]) for tile in TILES for i in range(MEMBERS)]
        far = {}
        for turn in (3, 2, 1):
            far[turn] = lax.ppermute(pieces[turn], "grp", turned(turn))
        return [pieces[0], far[1], far[2], far[3]]

    entry, own_plane, other_plane = call(
        entry_kernel, [VMEM] * 3, [VMEM] * 3,
        [f32(ROWS + 8, half), f32(PLANE, half), f32(PLANE, half)],
    )(first_level[None], coeffs[None], rows)
    other_next = to_previous(other_plane, 1)
    own_next = to_previous(own_plane, 0)
    other = lax.ppermute(entry, "grp", swap)
    *sent, meta = call(
        forth_kernel, [SMEM, SMEM] + [VMEM] * 5, [VMEM] * (MEMBERS + 1),
        [f32(SENT, chunk)] * MEMBERS + [f32(8, LANES)], flops=10**9,
    )(first_level, coeffs, forth, rows, own_next, other, other_next)
    got = through_tile(sent)

    parts = call(add_kernel, [VMEM] * MEMBERS, VMEM, f32(MEMBERS, TABLE, LANES), flops=10**8)(*got)
    for groups in (LINES, OTHER_LINES):
        parts = exchange(parts, groups)
        parts = call(total_kernel, [VMEM], VMEM, f32(MEMBERS, TABLE, LANES), flops=10**8)(parts)
    table = exchange(parts, LINES)
    picked = call(
        pick_kernel, [VMEM] * (MEMBERS + 1), [VMEM] * MEMBERS, [f32(FLAGS, chunk)] * MEMBERS, flops=10**8
    )(table, *got)
    final = through_tile(picked)

    other_out = call(
        other_back_kernel, [SMEM] + [VMEM] * (MEMBERS + 2), VMEM, f32(ROWS, half), flops=10**9
    )(first_level, meta, back, *final)
    swapped = lax.ppermute(other_out, "grp", swap)
    out = call(
        own_back_kernel, [SMEM] + [VMEM] * (MEMBERS + 2), HBM, f32(ROWS, width),
        (pltpu.VMEM((2 * MEMBERS, ROWS, chunk // 2), jnp.float32), DMA((2 * MEMBERS,))), flops=10**9,
    )(first_level, meta, back, *final)
    out = call(place_kernel, [VMEM, HBM], HBM, f32(ROWS, width), (DMA,), alias={1: 0})(swapped, out)
    return out[None]


def solution(mesh):
    in_specs = (P("grp", "slab", None), P("grp"), P("grp"), P("grp", "slab"))
    out_specs = P("grp", "slab", None)
    return jax.shard_map(shards, mesh=mesh, in_specs=in_specs, out_specs=out_specs, check_vma=False)
```

profile of v0, /device:TPU:1, one launch (start us, length us, event | category | flops | bytes accessed | tf_op | source)
XLA Modules:
  0.0 122.2 jit_solution(5846506033362143338)
XLA Ops:
  1.3 1.6 %copy-done = f32[1,128,4096]{2,1,0:T(8,128)S(1)} copy-done((f32[1,128,4096]{2,1,0:T(8,128)S(1)}, f32[1,128,4096]{2,1,0:T(8,128)}, u32[]{:S(2)}) %copy-start) | copy-done | bytes 2097176
  3.0 8.9 %collective-permute-start.1 = (f32[136,2048]{1,0:T(8,128)S(1)}, f32[136,2048]{1,0:T(8,128)S(1)}, u32[]{:S(2)}, u32[]{:S(2)}) collective-permute-start(f32[136,2048]{1,0:T(8,128)S(1)} %get-tuple-element.18), channel_id=1, source_target_pairs={{0,4},{4,0},{8,12},{12,8},{16,20},{20,16},{24,28},{28,24},{32,36},... | collective-permute-start | bytes 3342344 | tf_op jit(solution)/shard_map/ppermute | solution.py:339
  11.9 1.9 %collective-permute-start = (f32[8,2048]{1,0:T(8,128)S(1)}, f32[8,2048]{1,0:T(8,128)S(1)}, u32[]{:S(2)}, u32[]{:S(2)}) collective-permute-start(f32[8,2048]{1,0:T(8,128)S(1)} %get-tuple-element.17), channel_id=1, source_target_pairs={{0,3},{1,0},{2,1},{3,2},{4,7},{5,4},{6,5},{7,6},{8,11},{9,8},{10,9... | collective-permute-start | bytes 196616 | tf_op jit(solution)/shard_map/ppermute | solution.py:324
  13.8 1.9 %collective-permute-start.2 = (f32[8,2048]{1,0:T(8,128)S(1)}, f32[8,2048]{1,0:T(8,128)S(1)}, u32[]{:S(2)}, u32[]{:S(2)}) collective-permute-start(f32[8,2048]{1,0:T(8,128)S(1)} %get-tuple-element.19), channel_id=1, source_target_pairs={{0,7},{1,4},{2,5},{3,6},{4,3},{5,0},{6,1},{7,2},{8,15},{9,12},{10,... | collective-permute-start | bytes 196616 | tf_op jit(solution)/shard_map/ppermute | solution.py:324
  15.7 1.7 %collective-permute-done.own_next_ref = f32[8,2048]{1,0:T(8,128)S(1)} collective-permute-done((f32[8,2048]{1,0:T(8,128)S(1)}, f32[8,2048]{1,0:T(8,128)S(1)}, u32[]{:S(2)}, u32[]{:S(2)}) %collective-permute-start) | collective-permute-done | bytes 65568 | tf_op jit(solution)/shard_map/ppermute | solution.py:324
  17.4 2.1 %collective-permute-done.2.other_next_ref = f32[8,2048]{1,0:T(8,128)S(1)} collective-permute-done((f32[8,2048]{1,0:T(8,128)S(1)}, f32[8,2048]{1,0:T(8,128)S(1)}, u32[]{:S(2)}, u32[]{:S(2)}) %collective-permute-start.2) | collective-permute-done | bytes 65568 | tf_op jit(solution)/shard_map/ppermute | solution.py:324
  19.5 1.3 %shard_map.56 = (f32[240,512]{1,0:T(8,128)S(1)}, f32[240,512]{1,0:T(8,128)S(1)}, f32[240,512]{1,0:T(8,128)S(1)}, f32[240,512]{1,0:T(8,128)S(1)}, f32[8,128]{1,0:T(8,128)S(1)}) custom-call(s32[1]{0:T(128)} %copy.8.level_ref, s32[1]{0:T(128)} %copy.9.coeff_ref, bf16[9,240,272]{2,1,0:T(8,128)(2,1)S(1)} %copy-done.1, f32[128,4096]{1,0:T(8,128)S(1)} %bitcast.7, ...), custom_call_target="tpu_custom_call" | custom-call | flops 1000000000 | tf_op jit(solution)/shard_map/pallas_call | solution.py:340
  20.8 8.0 %collective-permute-start.3 = (f32[240,512]{1,0:T(8,128)S(1)}, f32[240,512]{1,0:T(8,128)S(1)}, u32[]{:S(2)}, u32[]{:S(2)}) collective-permute-start(f32[240,512]{1,0:T(8,128)S(1)} %get-tuple-element.22), channel_id=1, source_target_pairs={{0,8},{8,0},{64,72},{72,64},{16,24},{24,16},{80,88},{88,80},{32,40... | collective-permute-start | bytes 1474568 | tf_op jit(solution)/shard_map/ppermute | solution.py:330
  28.8 5.1 %collective-permute-start.4 = (f32[240,512]{1,0:T(8,128)S(1)}, f32[240,512]{1,0:T(8,128)S(1)}, u32[]{:S(2)}, u32[]{:S(2)}) collective-permute-start(f32[240,512]{1,0:T(8,128)S(1)} %get-tuple-element.23), channel_id=1, source_target_pairs={{0,64},{8,72},{64,0},{72,8},{16,80},{24,88},{80,16},{88,24},{32,96... | collective-permute-start | bytes 1474568 | tf_op jit(solution)/shard_map/ppermute | solution.py:330
  33.9 1.9 %collective-permute-start.5 = (f32[240,512]{1,0:T(8,128)S(1)}, f32[240,512]{1,0:T(8,128)S(1)}, u32[]{:S(2)}, u32[]{:S(2)}) collective-permute-start(f32[240,512]{1,0:T(8,128)S(1)} %get-tuple-element.24), channel_id=1, source_target_pairs={{0,72},{8,64},{64,8},{72,0},{16,88},{24,80},{80,24},{88,16},{32,10... | collective-permute-start | bytes 1474568 | tf_op jit(solution)/shard_map/ppermute | solution.py:330
  35.8 4.3 %collective-permute-done.4.refs_2_ = f32[240,512]{1,0:T(8,128)S(1)} collective-permute-done((f32[240,512]{1,0:T(8,128)S(1)}, f32[240,512]{1,0:T(8,128)S(1)}, u32[]{:S(2)}, u32[]{:S(2)}) %collective-permute-start.4) | collective-permute-done | bytes 491552 | tf_op jit(solution)/shard_map/ppermute | solution.py:330
  40.1 6.7 %collective-permute-done.5.refs_3_ = f32[240,512]{1,0:T(8,128)S(1)} collective-permute-done((f32[240,512]{1,0:T(8,128)S(1)}, f32[240,512]{1,0:T(8,128)S(1)}, u32[]{:S(2)}, u32[]{:S(2)}) %collective-permute-start.5) | collective-permute-done | bytes 491552 | tf_op jit(solution)/shard_map/ppermute | solution.py:330
  47.0 14.2 %all_to_all.15.got_ref = f32[4,264,128]{2,1,0:T(8,128)S(1)} all-to-all(f32[4,264,128]{2,1,0:T(8,128)S(1)} %shard_map.57), channel_id=1, replica_groups={{0,128,256,384},{8,136,264,392},{16,144,272,400},{24,152,280,408},{32,1..., dimensions={0} | all-to-all | bytes 1081344 | tf_op jit(solution)/shard_map/all_to_all | solution.py:288
  61.3 17.2 %all_to_all.16.got_ref = f32[4,264,128]{2,1,0:T(8,128)S(1)} all-to-all(f32[4,264,128]{2,1,0:T(8,128)S(1)} %shard_map.58), channel_id=1, replica_groups={{0,16,32,48},{64,80,96,112},{128,144,160,176},{192,208,224,240},{256,27..., dimensions={0} | all-to-all | bytes 1081344 | tf_op jit(solution)/shard_map/all_to_all | solution.py:288
  78.6 14.1 %all_to_all.17.table_ref = f32[4,264,128]{2,1,0:T(8,128)S(1)} all-to-all(f32[4,264,128]{2,1,0:T(8,128)S(1)} %shard_map.59), channel_id=1, replica_groups={{0,128,256,384},{8,136,264,392},{16,144,272,400},{24,152,280,408},{32,1..., dimensions={0} | all-to-all | bytes 1081344 | tf_op jit(solution)/shard_map/all_to_all | solution.py:288
  92.9 2.3 %collective-permute-start.6 = (f32[232,512]{1,0:T(8,128)S(1)}, f32[232,512]{1,0:T(8,128)S(1)}, u32[]{:S(2)}, u32[]{:S(2)}) collective-permute-start(f32[232,512]{1,0:T(8,128)S(1)} %get-tuple-element.26), channel_id=1, source_target_pairs={{0,8},{8,0},{64,72},{72,64},{16,24},{24,16},{80,88},{88,80},{32,40... | collective-permute-start | bytes 1425416 | tf_op jit(solution)/shard_map/ppermute | solution.py:330
  95.2 1.9 %collective-permute-start.7 = (f32[232,512]{1,0:T(8,128)S(1)}, f32[232,512]{1,0:T(8,128)S(1)}, u32[]{:S(2)}, u32[]{:S(2)}) collective-permute-start(f32[232,512]{1,0:T(8,128)S(1)} %get-tuple-element.27), channel_id=1, source_target_pairs={{0,64},{8,72},{64,0},{72,8},{16,80},{24,88},{80,16},{88,24},{32,96... | collective-permute-start | bytes 1425416 | tf_op jit(solution)/shard_map/ppermute | solution.py:330
  97.1 6.6 %collective-permute-start.8 = (f32[232,512]{1,0:T(8,128)S(1)}, f32[232,512]{1,0:T(8,128)S(1)}, u32[]{:S(2)}, u32[]{:S(2)}) collective-permute-start(f32[232,512]{1,0:T(8,128)S(1)} %get-tuple-element.28), channel_id=1, source_target_pairs={{0,72},{8,64},{64,8},{72,0},{16,88},{24,80},{80,24},{88,16},{32,10... | collective-permute-start | bytes 1425416 | tf_op jit(solution)/shard_map/ppermute | solution.py:330
  103.7 2.1 %collective-permute-done.7.refs_2_ = f32[232,512]{1,0:T(8,128)S(1)} collective-permute-done((f32[232,512]{1,0:T(8,128)S(1)}, f32[232,512]{1,0:T(8,128)S(1)}, u32[]{:S(2)}, u32[]{:S(2)}) %collective-permute-start.7) | collective-permute-done | bytes 475168 | tf_op jit(solution)/shard_map/ppermute | solution.py:330
  105.8 7.1 %collective-permute-done.8.refs_3_ = f32[232,512]{1,0:T(8,128)S(1)} collective-permute-done((f32[232,512]{1,0:T(8,128)S(1)}, f32[232,512]{1,0:T(8,128)S(1)}, u32[]{:S(2)}, u32[]{:S(2)}) %collective-permute-start.8) | collective-permute-done | bytes 475168 | tf_op jit(solution)/shard_map/ppermute | solution.py:330
  113.5 5.5 %collective-permute-start.9 = (f32[128,2048]{1,0:T(8,128)S(1)}, f32[128,2048]{1,0:T(8,128)S(1)}, u32[]{:S(2)}, u32[]{:S(2)}) collective-permute-start(f32[128,2048]{1,0:T(8,128)S(1)} %shard_map.61), channel_id=1, source_target_pairs={{0,4},{4,0},{8,12},{12,8},{16,20},{20,16},{24,28},{28,24},{32,36},... | collective-permute-start | bytes 3145736 | tf_op jit(solution)/shard_map/ppermute | solution.py:359
  118.9 1.4 %shard_map.62.filled_ref = f32[128,4096]{1,0:T(8,128)} custom-call(s32[1]{0:T(128)} %copy.8.level_ref, f32[8,128]{1,0:T(8,128)S(1)} %get-tuple-element.20.meta_ref, bf16[9,128,232]{2,1,0:T(8,128)(2,1)S(1)} %copy-done.2, f32[232,512]{1,0:T(8,128)S(1)} %get-tuple-element.25.refs_0_, f32[232,512]{1,0:T(8,128)S(1)} %collective-permute-done.6.refs_1_, ...), custom_call_target="tpu_custom_call" | custom-call | flops 1000000000 | tf_op jit(solution)/shard_map/pallas_call | solution.py:360
  120.3 0.9 collective-permute-done.9.values_ref
  121.2 1.0 shard_map.63
  (14 shorter events, 1.2 us)
Async XLA Ops:
  1.3 1.6 %copy-start = (f32[1,128,4096]{2,1,0:T(8,128)S(1)}, f32[1,128,4096]{2,1,0:T(8,128)}, u32[]{:S(2)}) copy-start(f32[1,128,4096]{2,1,0:T(8,128)} %param.6) | copy-start | bytes 6291460
  2.9 16.6 %copy-start.1 = (bf16[9,240,272]{2,1,0:T(8,128)(2,1)S(1)}, bf16[9,240,272]{2,1,0:T(8,128)(2,1)}, u32[]{:S(2)}) copy-start(bf16[9,240,272]{2,1,0:T(8,128)(2,1)} %constant.4.clone.table_ref) | copy-start | bytes 3525124
  3.0 16.5 %collective-permute-start.1 = (f32[136,2048]{1,0:T(8,128)S(1)}, f32[136,2048]{1,0:T(8,128)S(1)}, u32[]{:S(2)}, u32[]{:S(2)}) collective-permute-start(f32[136,2048]{1,0:T(8,128)S(1)} %get-tuple-element.18), channel_id=1, source_target_pairs={{0,4},{4,0},{8,12},{12,8},{16,20},{20,16},{24,28},{28,24},{32,36},... | collective-permute-start | bytes 3342344 | tf_op jit(solution)/shard_map/ppermute | solution.py:339
  11.9 5.5 %collective-permute-start = (f32[8,2048]{1,0:T(8,128)S(1)}, f32[8,2048]{1,0:T(8,128)S(1)}, u32[]{:S(2)}, u32[]{:S(2)}) collective-permute-start(f32[8,2048]{1,0:T(8,128)S(1)} %get-tuple-element.17), channel_id=1, source_target_pairs={{0,3},{1,0},{2,1},{3,2},{4,7},{5,4},{6,5},{7,6},{8,11},{9,8},{10,9... | collective-permute-start | bytes 196616 | tf_op jit(solution)/shard_map/ppermute | solution.py:324
  13.8 5.7 %collective-permute-start.2 = (f32[8,2048]{1,0:T(8,128)S(1)}, f32[8,2048]{1,0:T(8,128)S(1)}, u32[]{:S(2)}, u32[]{:S(2)}) collective-permute-start(f32[8,2048]{1,0:T(8,128)S(1)} %get-tuple-element.19), channel_id=1, source_target_pairs={{0,7},{1,4},{2,5},{3,6},{4,3},{5,0},{6,1},{7,2},{8,15},{9,12},{10,... | collective-permute-start | bytes 196616 | tf_op jit(solution)/shard_map/ppermute | solution.py:324
  20.8 15.0 %collective-permute-start.3 = (f32[240,512]{1,0:T(8,128)S(1)}, f32[240,512]{1,0:T(8,128)S(1)}, u32[]{:S(2)}, u32[]{:S(2)}) collective-permute-start(f32[240,512]{1,0:T(8,128)S(1)} %get-tuple-element.22), channel_id=1, source_target_pairs={{0,8},{8,0},{64,72},{72,64},{16,24},{24,16},{80,88},{88,80},{32,40... | collective-permute-start | bytes 1474568 | tf_op jit(solution)/shard_map/ppermute | solution.py:330
  28.8 11.3 %collective-permute-start.4 = (f32[240,512]{1,0:T(8,128)S(1)}, f32[240,512]{1,0:T(8,128)S(1)}, u32[]{:S(2)}, u32[]{:S(2)}) collective-permute-start(f32[240,512]{1,0:T(8,128)S(1)} %get-tuple-element.23), channel_id=1, source_target_pairs={{0,64},{8,72},{64,0},{72,8},{16,80},{24,88},{80,16},{88,24},{32,96... | collective-permute-start | bytes 1474568 | tf_op jit(solution)/shard_map/ppermute | solution.py:330
  33.9 12.9 %collective-permute-start.5 = (f32[240,512]{1,0:T(8,128)S(1)}, f32[240,512]{1,0:T(8,128)S(1)}, u32[]{:S(2)}, u32[]{:S(2)}) collective-permute-start(f32[240,512]{1,0:T(8,128)S(1)} %get-tuple-element.24), channel_id=1, source_target_pairs={{0,72},{8,64},{64,8},{72,0},{16,88},{24,80},{80,24},{88,16},{32,10... | collective-permute-start | bytes 1474568 | tf_op jit(solution)/shard_map/ppermute | solution.py:330
  78.5 34.3 %copy-start.2 = (bf16[9,128,232]{2,1,0:T(8,128)(2,1)S(1)}, bf16[9,128,232]{2,1,0:T(8,128)(2,1)}, u32[]{:S(2)}) copy-start(bf16[9,128,232]{2,1,0:T(8,128)(2,1)} %constant.5.clone.table_ref) | copy-start | bytes 1603588
  92.9 10.8 %collective-permute-start.6 = (f32[232,512]{1,0:T(8,128)S(1)}, f32[232,512]{1,0:T(8,128)S(1)}, u32[]{:S(2)}, u32[]{:S(2)}) collective-permute-start(f32[232,512]{1,0:T(8,128)S(1)} %get-tuple-element.26), channel_id=1, source_target_pairs={{0,8},{8,0},{64,72},{72,64},{16,24},{24,16},{80,88},{88,80},{32,40... | collective-permute-start | bytes 1425416 | tf_op jit(solution)/shard_map/ppermute | solution.py:330
  95.2 10.6 %collective-permute-start.7 = (f32[232,512]{1,0:T(8,128)S(1)}, f32[232,512]{1,0:T(8,128)S(1)}, u32[]{:S(2)}, u32[]{:S(2)}) collective-permute-start(f32[232,512]{1,0:T(8,128)S(1)} %get-tuple-element.27), channel_id=1, source_target_pairs={{0,64},{8,72},{64,0},{72,8},{16,80},{24,88},{80,16},{88,24},{32,96... | collective-permute-start | bytes 1425416 | tf_op jit(solution)/shard_map/ppermute | solution.py:330
  97.1 15.8 %collective-permute-start.8 = (f32[232,512]{1,0:T(8,128)S(1)}, f32[232,512]{1,0:T(8,128)S(1)}, u32[]{:S(2)}, u32[]{:S(2)}) collective-permute-start(f32[232,512]{1,0:T(8,128)S(1)} %get-tuple-element.28), channel_id=1, source_target_pairs={{0,72},{8,64},{64,8},{72,0},{16,88},{24,80},{80,24},{88,16},{32,10... | collective-permute-start | bytes 1425416 | tf_op jit(solution)/shard_map/ppermute | solution.py:330
  113.5 7.7 %collective-permute-start.9 = (f32[128,2048]{1,0:T(8,128)S(1)}, f32[128,2048]{1,0:T(8,128)S(1)}, u32[]{:S(2)}, u32[]{:S(2)}) collective-permute-start(f32[128,2048]{1,0:T(8,128)S(1)} %shard_map.61), channel_id=1, source_target_pairs={{0,4},{4,0},{8,12},{12,8},{16,20},{20,16},{24,28},{28,24},{32,36},... | collective-permute-start | bytes 3145736 | tf_op jit(solution)/shard_map/ppermute | solution.py:359
where the time goes:
time: 123 us; the launch traced here: 122 us
  blocking collectives  45.6 us (37%)
  starting transfers between devices  44 us (36%)
  waiting for transfers between devices  24.8 us (20%)
  Pallas kernels  4.81 us (4%)
  local copies, waits for them, and re-layouts  1.59 us (1%)
  between operations  1.46 us (1%)
    all_to_all x3, blocking collectives, exchange(): lax.all_to_all(values, 'grp', 0, 0, axis_index_groups=groups, tiled=True)  45.6 us
    ppermute x6, starting transfers between devices, through_tile(): far[turn] = lax.ppermute(pieces[turn], 'grp', turned(turn))  25.8 us
    ppermute x6, waiting for transfers between devices, through_tile(): far[turn] = lax.ppermute(pieces[turn], 'grp', turned(turn))  20.1 us
    ppermute x1, starting transfers between devices, shards(): other = lax.ppermute(entry, 'grp', swap)  8.88 us
    ppermute x1, starting transfers between devices, shards(): swapped = lax.ppermute(other_out, 'grp', swap)  5.45 us
    ppermute x2, starting transfers between devices, to_previous(): return lax.ppermute(values, ('grp', 'slab'), pairs)  3.84 us
    ppermute x2, waiting for transfers between devices, to_previous(): return lax.ppermute(values, ('grp', 'slab'), pairs)  3.78 us
  transfers between devices with their start and end apart: 10, of which 7 were waited for; matrix products, arithmetic and copies ran while one was open for 0% of the time, Pallas kernels for 1%

commit v1 on v0

--- a/solution.py
+++ b/solution.py
@@ -23,6 +23,7 @@
 ENTRY = 2 * (ROWS + PLANE)
 TABLE = 8 * BLOCK + PLANE
 LANES = 128
+SHARE = 16
 
 
 def slots_of(levels):
@@ -130,20 +131,22 @@
     return ref.at[rows, pl.ds(pl.multiple_of(core * width, LANES), width)]
 
 
-def entry_kernel(level_ref, coeff_ref, rows_ref, out_ref, own_ref, other_ref):
+def entry_kernel(rows_ref, out_ref, own_plane_ref, other_plane_ref):
     core = core_here()
     half = out_ref.shape[1]
     mine = pl.ds(pl.multiple_of(core * half, LANES), half)
     theirs = pl.ds(pl.multiple_of((1 - core) * half, LANES), half)
-    own_ref[...] = rows_ref[:PLANE, mine]
-    other_ref[...] = rows_ref[:PLANE, theirs]
+    own_plane_ref[...] = rows_ref[:PLANE, mine]
+    other_plane_ref[...] = rows_ref[:PLANE, theirs]
     out_ref[:ROWS, :] = rows_ref[:, theirs]
-    line = lax.broadcasted_iota(jnp.int32, (8, half), 0)
-    out_ref[ROWS:, :] = jnp.where(line == 0, level_ref[...], coeff_ref[...]).astype(jnp.float32)
-
-
-def forth_kernel(level_ref, coeff_ref, table_ref, rows_ref, own_next_ref, other_ref, other_next_ref, *outs):
-    *out_refs, meta_ref = outs
+
+
+def stamp_kernel(level_ref, coeff_ref, rows_ref, out_ref):
+    line = lax.broadcasted_iota(jnp.int32, (8, out_ref.shape[1]), 0)
+    out_ref[ROWS:, :] = jnp.where(line == 0, level_ref[0], coeff_ref[0]).astype(jnp.float32)
+
+
+def forth_kernel(turns, level_ref, coeff_ref, table_ref, rows_ref, own_next_ref, other_ref, other_next_ref, *out_refs):
     own_level = level_ref[0]
     other_level = number_in(other_ref, ROWS).astype(jnp.int32)
     which = (own_level - LOW_LEVEL) * 3 + other_level - LOW_LEVEL
@@ -157,7 +160,7 @@
     line = lax.broadcasted_iota(jnp.int32, (SENT - FLAGS, width), 0)
     flags = jnp.where(line == 0, six, eight)
     first = core_here() * MEMBERS * chunk
-    for turn, out_ref in enumerate(out_refs):
+    for turn, out_ref in zip(turns, out_refs):
         for h in range(2):
             here = slice(h * width, (h + 1) * width)
             low = piece_here(turn) * chunk + h * width
@@ -168,6 +171,9 @@
             )
             out_ref[:, here] = two_part_dot(table, values)
             out_ref[FLAGS:SENT, here] = flags
+
+
+def meta_kernel(other_ref, meta_ref):
     meta_ref[...] = other_ref[ROWS:, :LANES]
 
 
@@ -258,10 +264,16 @@
         copy.wait()
 
 
-def place_kernel(values_ref, filled_ref, out_ref, sem):
-    copy = pltpu.make_async_copy(values_ref, half_of(out_ref, 1 - core_here()), sem)
-    copy.start()
-    copy.wait()
+def place_kernel(values_ref, filled_ref, out_ref, sems):
+    copies = []
+    for i in range(ROWS // SHARE):
+        part = slice(i * SHARE, (i + 1) * SHARE)
+        to = half_of(out_ref, 1 - core_here(), part)
+        copies.append(pltpu.make_async_copy(values_ref.at[part], to, sems.at[i]))
+    for copy in copies:
+        copy.start()
+    for copy in copies:
+        copy.wait()
 
 
 def member(y, z, core):
@@ -331,17 +343,24 @@
         return [pieces[0], far[1], far[2], far[3]]
 
     entry, own_plane, other_plane = call(
-        entry_kernel, [VMEM] * 3, [VMEM] * 3,
+        entry_kernel, [VMEM], [VMEM] * 3,
         [f32(ROWS + 8, half), f32(PLANE, half), f32(PLANE, half)],
-    )(first_level[None], coeffs[None], rows)
+    )(rows)
     other_next = to_previous(other_plane, 1)
     own_next = to_previous(own_plane, 0)
+    entry = call(stamp_kernel, [SMEM, SMEM, VMEM], VMEM, f32(ROWS + 8, half), alias={2: 0})(first_level, coeffs, entry)
     other = lax.ppermute(entry, "grp", swap)
-    *sent, meta = call(
-        forth_kernel, [SMEM, SMEM] + [VMEM] * 5, [VMEM] * (MEMBERS + 1),
-        [f32(SENT, chunk)] * MEMBERS + [f32(8, LANES)], flops=10**9,
-    )(first_level, coeffs, forth, rows, own_next, other, other_next)
-    got = through_tile(sent)
+
+    def surplus(*turns):
+        return call(
+            functools.partial(forth_kernel, turns), [SMEM, SMEM] + [VMEM] * 5, [VMEM] * len(turns),
+            [f32(SENT, chunk)] * len(turns), flops=10**9,
+        )(first_level, coeffs, forth, rows, own_next, other, other_next)
+
+    sent = surplus(1, 2, 3)
+    (stays,) = surplus(0)
+    meta = call(meta_kernel, [VMEM], VMEM, f32(8, LANES))(other)
+    got = through_tile([stays, *sent])
 
     parts = call(add_kernel, [VMEM] * MEMBERS, VMEM, f32(MEMBERS, TABLE, LANES), flops=10**8)(*got)
     for groups in (LINES, OTHER_LINES):
@@ -361,7 +380,7 @@
         own_back_kernel, [SMEM] + [VMEM] * (MEMBERS + 2), HBM, f32(ROWS, width),
         (pltpu.VMEM((2 * MEMBERS, ROWS, chunk // 2), jnp.float32), DMA((2 * MEMBERS,))), flops=10**9,
     )(first_level, meta, back, *final)
-    out = call(place_kernel, [VMEM, HBM], HBM, f32(ROWS, width), (DMA,), alias={1: 0})(swapped, out)
+    out = call(place_kernel, [VMEM, HBM], HBM, f32(ROWS, width), (DMA((ROWS // SHARE,)),), alias={1: 0})(swapped, out)
     return out[None]
 
 

time: 123 us -> 122 us (level)
    pallas_call x3 -> x6, Pallas kernels: 2.34 us -> 2.63 us  [the longest x2 1.51 us: surplus(): call(functools.partial(forth_kernel, turns), [SMEM, SMEM] + [VMEM] * 5, [...]
  transfers between devices with their start and end apart: 10 -> 10, of which waited for: 7 -> 7; matrix products, arithmetic and copies ran while one was open for 0% -> 0% of each run, Pallas kernels for 1% -> 2%
where the time goes in v1:
time: 122 us
  blocking collectives  45.1 us (37%)
  starting transfers between devices  44.4 us (36%)
  waiting for transfers between devices  24.3 us (20%)
  Pallas kernels  5.06 us (4%)
  local copies, waits for them, and re-layouts  1.6 us (1%)
  between operations  1.48 us (1%)
    all_to_all x3, blocking collectives, exchange(): lax.all_to_all(values, 'grp', 0, 0, axis_index_groups=groups, tiled=True)  45.1 us
    ppermute x6, starting transfers between devices, through_tile(): far[turn] = lax.ppermute(pieces[turn], 'grp', turned(turn))  25.8 us
    ppermute x6, waiting for transfers between devices, through_tile(): far[turn] = lax.ppermute(pieces[turn], 'grp', turned(turn))  19.6 us
    ppermute x1, starting transfers between devices, shards(): other = lax.ppermute(entry, 'grp', swap)  9.01 us
    ppermute x1, starting transfers between devices, shards(): swapped = lax.ppermute(other_out, 'grp', swap)  5.8 us
    ppermute x2, starting transfers between devices, to_previous(): return lax.ppermute(values, ('grp', 'slab'), pairs)  3.84 us
    ppermute x2, waiting for transfers between devices, to_previous(): return lax.ppermute(values, ('grp', 'slab'), pairs)  3.78 us
  transfers between devices with their start and end apart: 10, of which 7 were waited for; matrix products, arithmetic and copies ran while one was open for 0% of the time, Pallas kernels for 2%

profile of v1, /device:TPU:1, one launch (start us, length us, event | category | flops | bytes accessed | tf_op | source)
XLA Modules:
  0.0 121.9 jit_solution(4160840625830097027)
XLA Ops:
  1.3 1.6 %copy-done = f32[1,128,4096]{2,1,0:T(8,128)S(1)} copy-done((f32[1,128,4096]{2,1,0:T(8,128)S(1)}, f32[1,128,4096]{2,1,0:T(8,128)}, u32[]{:S(2)}) %copy-start) | copy-done | bytes 2097176
  3.0 9.0 %collective-permute-start = (f32[136,2048]{1,0:T(8,128)S(1)}, f32[136,2048]{1,0:T(8,128)S(1)}, u32[]{:S(2)}, u32[]{:S(2)}) collective-permute-start(f32[136,2048]{1,0:T(8,128)S(1)} %shard_map.56), channel_id=1, source_target_pairs={{0,4},{4,0},{8,12},{12,8},{16,20},{20,16},{24,28},{28,24},{32,36},... | collective-permute-start | bytes 3342344 | tf_op jit(solution)/shard_map/ppermute | solution.py:352
  12.0 1.9 %collective-permute-start.1 = (f32[8,2048]{1,0:T(8,128)S(1)}, f32[8,2048]{1,0:T(8,128)S(1)}, u32[]{:S(2)}, u32[]{:S(2)}) collective-permute-start(f32[8,2048]{1,0:T(8,128)S(1)} %get-tuple-element.16), channel_id=1, source_target_pairs={{0,3},{1,0},{2,1},{3,2},{4,7},{5,4},{6,5},{7,6},{8,11},{9,8},{10,9... | collective-permute-start | bytes 196616 | tf_op jit(solution)/shard_map/ppermute | solution.py:336
  13.9 1.9 %collective-permute-start.2 = (f32[8,2048]{1,0:T(8,128)S(1)}, f32[8,2048]{1,0:T(8,128)S(1)}, u32[]{:S(2)}, u32[]{:S(2)}) collective-permute-start(f32[8,2048]{1,0:T(8,128)S(1)} %get-tuple-element.17), channel_id=1, source_target_pairs={{0,7},{1,4},{2,5},{3,6},{4,3},{5,0},{6,1},{7,2},{8,15},{9,12},{10,... | collective-permute-start | bytes 196616 | tf_op jit(solution)/shard_map/ppermute | solution.py:336
  15.9 1.7 %collective-permute-done.1.own_next_ref = f32[8,2048]{1,0:T(8,128)S(1)} collective-permute-done((f32[8,2048]{1,0:T(8,128)S(1)}, f32[8,2048]{1,0:T(8,128)S(1)}, u32[]{:S(2)}, u32[]{:S(2)}) %collective-permute-start.1) | collective-permute-done | bytes 65568 | tf_op jit(solution)/shard_map/ppermute | solution.py:336
  17.5 2.1 %collective-permute-done.2.other_next_ref = f32[8,2048]{1,0:T(8,128)S(1)} collective-permute-done((f32[8,2048]{1,0:T(8,128)S(1)}, f32[8,2048]{1,0:T(8,128)S(1)}, u32[]{:S(2)}, u32[]{:S(2)}) %collective-permute-start.2) | collective-permute-done | bytes 65568 | tf_op jit(solution)/shard_map/ppermute | solution.py:336
  19.7 1.0 shard_map.59
  20.7 8.0 %collective-permute-start.3 = (f32[240,512]{1,0:T(8,128)S(1)}, f32[240,512]{1,0:T(8,128)S(1)}, u32[]{:S(2)}, u32[]{:S(2)}) collective-permute-start(f32[240,512]{1,0:T(8,128)S(1)} %get-tuple-element.18), channel_id=1, source_target_pairs={{0,8},{8,0},{64,72},{72,64},{16,24},{24,16},{80,88},{88,80},{32,40... | collective-permute-start | bytes 1474568 | tf_op jit(solution)/shard_map/ppermute | solution.py:342
  28.7 5.1 %collective-permute-start.4 = (f32[240,512]{1,0:T(8,128)S(1)}, f32[240,512]{1,0:T(8,128)S(1)}, u32[]{:S(2)}, u32[]{:S(2)}) collective-permute-start(f32[240,512]{1,0:T(8,128)S(1)} %get-tuple-element.19), channel_id=1, source_target_pairs={{0,64},{8,72},{64,0},{72,8},{16,80},{24,88},{80,16},{88,24},{32,96... | collective-permute-start | bytes 1474568 | tf_op jit(solution)/shard_map/ppermute | solution.py:342
  33.8 1.9 %collective-permute-start.5 = (f32[240,512]{1,0:T(8,128)S(1)}, f32[240,512]{1,0:T(8,128)S(1)}, u32[]{:S(2)}, u32[]{:S(2)}) collective-permute-start(f32[240,512]{1,0:T(8,128)S(1)} %get-tuple-element.20), channel_id=1, source_target_pairs={{0,72},{8,64},{64,8},{72,0},{16,88},{24,80},{80,24},{88,16},{32,10... | collective-permute-start | bytes 1474568 | tf_op jit(solution)/shard_map/ppermute | solution.py:342
  36.2 3.8 %collective-permute-done.4.refs_2_ = f32[240,512]{1,0:T(8,128)S(1)} collective-permute-done((f32[240,512]{1,0:T(8,128)S(1)}, f32[240,512]{1,0:T(8,128)S(1)}, u32[]{:S(2)}, u32[]{:S(2)}) %collective-permute-start.4) | collective-permute-done | bytes 491552 | tf_op jit(solution)/shard_map/ppermute | solution.py:342
  40.0 6.7 %collective-permute-done.5.refs_3_ = f32[240,512]{1,0:T(8,128)S(1)} collective-permute-done((f32[240,512]{1,0:T(8,128)S(1)}, f32[240,512]{1,0:T(8,128)S(1)}, u32[]{:S(2)}, u32[]{:S(2)}) %collective-permute-start.5) | collective-permute-done | bytes 491552 | tf_op jit(solution)/shard_map/ppermute | solution.py:342
  46.9 14.2 %all_to_all.15.got_ref = f32[4,264,128]{2,1,0:T(8,128)S(1)} all-to-all(f32[4,264,128]{2,1,0:T(8,128)S(1)} %shard_map.60), channel_id=1, replica_groups={{0,128,256,384},{8,136,264,392},{16,144,272,400},{24,152,280,408},{32,1..., dimensions={0} | all-to-all | bytes 1081344 | tf_op jit(solution)/shard_map/all_to_all | solution.py:300
  61.2 17.2 %all_to_all.16.got_ref = f32[4,264,128]{2,1,0:T(8,128)S(1)} all-to-all(f32[4,264,128]{2,1,0:T(8,128)S(1)} %shard_map.61), channel_id=1, replica_groups={{0,16,32,48},{64,80,96,112},{128,144,160,176},{192,208,224,240},{256,27..., dimensions={0} | all-to-all | bytes 1081344 | tf_op jit(solution)/shard_map/all_to_all | solution.py:300
  78.5 13.6 %all_to_all.17.table_ref = f32[4,264,128]{2,1,0:T(8,128)S(1)} all-to-all(f32[4,264,128]{2,1,0:T(8,128)S(1)} %shard_map.62), channel_id=1, replica_groups={{0,128,256,384},{8,136,264,392},{16,144,272,400},{24,152,280,408},{32,1..., dimensions={0} | all-to-all | bytes 1081344 | tf_op jit(solution)/shard_map/all_to_all | solution.py:300
  92.2 2.6 %collective-permute-start.6 = (f32[232,512]{1,0:T(8,128)S(1)}, f32[232,512]{1,0:T(8,128)S(1)}, u32[]{:S(2)}, u32[]{:S(2)}) collective-permute-start(f32[232,512]{1,0:T(8,128)S(1)} %get-tuple-element.22), channel_id=1, source_target_pairs={{0,8},{8,0},{64,72},{72,64},{16,24},{24,16},{80,88},{88,80},{32,40... | collective-permute-start | bytes 1425416 | tf_op jit(solution)/shard_map/ppermute | solution.py:342
  94.9 1.9 %collective-permute-start.7 = (f32[232,512]{1,0:T(8,128)S(1)}, f32[232,512]{1,0:T(8,128)S(1)}, u32[]{:S(2)}, u32[]{:S(2)}) collective-permute-start(f32[232,512]{1,0:T(8,128)S(1)} %get-tuple-element.23), channel_id=1, source_target_pairs={{0,64},{8,72},{64,0},{72,8},{16,80},{24,88},{80,16},{88,24},{32,96... | collective-permute-start | bytes 1425416 | tf_op jit(solution)/shard_map/ppermute | solution.py:342
  96.8 6.2 %collective-permute-start.8 = (f32[232,512]{1,0:T(8,128)S(1)}, f32[232,512]{1,0:T(8,128)S(1)}, u32[]{:S(2)}, u32[]{:S(2)}) collective-permute-start(f32[232,512]{1,0:T(8,128)S(1)} %get-tuple-element.24), channel_id=1, source_target_pairs={{0,72},{8,64},{64,8},{72,0},{16,88},{24,80},{80,24},{88,16},{32,10... | collective-permute-start | bytes 1425416 | tf_op jit(solution)/shard_map/ppermute | solution.py:342
  103.1 2.4 %collective-permute-done.7.refs_2_ = f32[232,512]{1,0:T(8,128)S(1)} collective-permute-done((f32[232,512]{1,0:T(8,128)S(1)}, f32[232,512]{1,0:T(8,128)S(1)}, u32[]{:S(2)}, u32[]{:S(2)}) %collective-permute-start.7) | collective-permute-done | bytes 475168 | tf_op jit(solution)/shard_map/ppermute | solution.py:342
  105.5 6.8 %collective-permute-done.8.refs_3_ = f32[232,512]{1,0:T(8,128)S(1)} collective-permute-done((f32[232,512]{1,0:T(8,128)S(1)}, f32[232,512]{1,0:T(8,128)S(1)}, u32[]{:S(2)}, u32[]{:S(2)}) %collective-permute-start.8) | collective-permute-done | bytes 475168 | tf_op jit(solution)/shard_map/ppermute | solution.py:342
  112.8 5.8 %collective-permute-start.9 = (f32[128,2048]{1,0:T(8,128)S(1)}, f32[128,2048]{1,0:T(8,128)S(1)}, u32[]{:S(2)}, u32[]{:S(2)}) collective-permute-start(f32[128,2048]{1,0:T(8,128)S(1)} %shard_map.64), channel_id=1, source_target_pairs={{0,4},{4,0},{8,12},{12,8},{16,20},{20,16},{24,28},{28,24},{32,36},... | collective-permute-start | bytes 3145736 | tf_op jit(solution)/shard_map/ppermute | solution.py:378
  118.7 1.4 %shard_map.65.filled_ref = f32[128,4096]{1,0:T(8,128)} custom-call(s32[1]{0:T(128)S(6)} %copy.10.level_ref, f32[8,128]{1,0:T(8,128)S(1)} %shard_map.57.meta_ref, bf16[9,128,232]{2,1,0:T(8,128)(2,1)S(1)} %copy-done.3, f32[232,512]{1,0:T(8,128)S(1)} %get-tuple-element.21.refs_0_, f32[232,512]{1,0:T(8,128)S(1)} %collective-permute-done.6.refs_1_, ...), custom_call_target="tpu_custom_call" | custom-call | flops 1000000000 | tf_op jit(solution)/shard_map/pallas_call | solution.py:379
  120.0 0.9 collective-permute-done.9.values_ref
  120.9 1.0 shard_map.66
  (19 shorter events, 1.6 us)
Async XLA Ops:
  1.3 1.6 %copy-start = (f32[1,128,4096]{2,1,0:T(8,128)S(1)}, f32[1,128,4096]{2,1,0:T(8,128)}, u32[]{:S(2)}) copy-start(f32[1,128,4096]{2,1,0:T(8,128)} %param.6) | copy-start | bytes 6291460
  2.9 16.8 %copy-start.1 = (f32[1,128,4096]{2,1,0:T(8,128)S(1)}, f32[1,128,4096]{2,1,0:T(8,128)}, u32[]{:S(2)}) copy-start(f32[1,128,4096]{2,1,0:T(8,128)} %param.6) | copy-start | bytes 6291460
  2.9 16.8 %copy-start.2 = (bf16[9,240,272]{2,1,0:T(8,128)(2,1)S(1)}, bf16[9,240,272]{2,1,0:T(8,128)(2,1)}, u32[]{:S(2)}) copy-start(bf16[9,240,272]{2,1,0:T(8,128)(2,1)} %constant.4.clone.table_ref) | copy-start | bytes 3525124
  3.0 16.7 %collective-permute-start = (f32[136,2048]{1,0:T(8,128)S(1)}, f32[136,2048]{1,0:T(8,128)S(1)}, u32[]{:S(2)}, u32[]{:S(2)}) collective-permute-start(f32[136,2048]{1,0:T(8,128)S(1)} %shard_map.56), channel_id=1, source_target_pairs={{0,4},{4,0},{8,12},{12,8},{16,20},{20,16},{24,28},{28,24},{32,36},... | collective-permute-start | bytes 3342344 | tf_op jit(solution)/shard_map/ppermute | solution.py:352
  12.0 5.5 %collective-permute-start.1 = (f32[8,2048]{1,0:T(8,128)S(1)}, f32[8,2048]{1,0:T(8,128)S(1)}, u32[]{:S(2)}, u32[]{:S(2)}) collective-permute-start(f32[8,2048]{1,0:T(8,128)S(1)} %get-tuple-element.16), channel_id=1, source_target_pairs={{0,3},{1,0},{2,1},{3,2},{4,7},{5,4},{6,5},{7,6},{8,11},{9,8},{10,9... | collective-permute-start | bytes 196616 | tf_op jit(solution)/shard_map/ppermute | solution.py:336
  13.9 5.7 %collective-permute-start.2 = (f32[8,2048]{1,0:T(8,128)S(1)}, f32[8,2048]{1,0:T(8,128)S(1)}, u32[]{:S(2)}, u32[]{:S(2)}) collective-permute-start(f32[8,2048]{1,0:T(8,128)S(1)} %get-tuple-element.17), channel_id=1, source_target_pairs={{0,7},{1,4},{2,5},{3,6},{4,3},{5,0},{6,1},{7,2},{8,15},{9,12},{10,... | collective-permute-start | bytes 196616 | tf_op jit(solution)/shard_map/ppermute | solution.py:336
  20.7 15.5 %collective-permute-start.3 = (f32[240,512]{1,0:T(8,128)S(1)}, f32[240,512]{1,0:T(8,128)S(1)}, u32[]{:S(2)}, u32[]{:S(2)}) collective-permute-start(f32[240,512]{1,0:T(8,128)S(1)} %get-tuple-element.18), channel_id=1, source_target_pairs={{0,8},{8,0},{64,72},{72,64},{16,24},{24,16},{80,88},{88,80},{32,40... | collective-permute-start | bytes 1474568 | tf_op jit(solution)/shard_map/ppermute | solution.py:342
  28.7 11.3 %collective-permute-start.4 = (f32[240,512]{1,0:T(8,128)S(1)}, f32[240,512]{1,0:T(8,128)S(1)}, u32[]{:S(2)}, u32[]{:S(2)}) collective-permute-start(f32[240,512]{1,0:T(8,128)S(1)} %get-tuple-element.19), channel_id=1, source_target_pairs={{0,64},{8,72},{64,0},{72,8},{16,80},{24,88},{80,16},{88,24},{32,96... | collective-permute-start | bytes 1474568 | tf_op jit(solution)/shard_map/ppermute | solution.py:342
  33.8 12.9 %collective-permute-start.5 = (f32[240,512]{1,0:T(8,128)S(1)}, f32[240,512]{1,0:T(8,128)S(1)}, u32[]{:S(2)}, u32[]{:S(2)}) collective-permute-start(f32[240,512]{1,0:T(8,128)S(1)} %get-tuple-element.20), channel_id=1, source_target_pairs={{0,72},{8,64},{64,8},{72,0},{16,88},{24,80},{80,24},{88,16},{32,10... | collective-permute-start | bytes 1474568 | tf_op jit(solution)/shard_map/ppermute | solution.py:342
  92.1 20.2 %copy-start.3 = (bf16[9,128,232]{2,1,0:T(8,128)(2,1)S(1)}, bf16[9,128,232]{2,1,0:T(8,128)(2,1)}, u32[]{:S(2)}) copy-start(bf16[9,128,232]{2,1,0:T(8,128)(2,1)} %constant.5.clone.table_ref) | copy-start | bytes 1603588
  92.2 10.8 %collective-permute-start.6 = (f32[232,512]{1,0:T(8,128)S(1)}, f32[232,512]{1,0:T(8,128)S(1)}, u32[]{:S(2)}, u32[]{:S(2)}) collective-permute-start(f32[232,512]{1,0:T(8,128)S(1)} %get-tuple-element.22), channel_id=1, source_target_pairs={{0,8},{8,0},{64,72},{72,64},{16,24},{24,16},{80,88},{88,80},{32,40... | collective-permute-start | bytes 1425416 | tf_op jit(solution)/shard_map/ppermute | solution.py:342
  94.9 10.6 %collective-permute-start.7 = (f32[232,512]{1,0:T(8,128)S(1)}, f32[232,512]{1,0:T(8,128)S(1)}, u32[]{:S(2)}, u32[]{:S(2)}) collective-permute-start(f32[232,512]{1,0:T(8,128)S(1)} %get-tuple-element.23), channel_id=1, source_target_pairs={{0,64},{8,72},{64,0},{72,8},{16,80},{24,88},{80,16},{88,24},{32,96... | collective-permute-start | bytes 1425416 | tf_op jit(solution)/shard_map/ppermute | solution.py:342
  96.8 15.4 %collective-permute-start.8 = (f32[232,512]{1,0:T(8,128)S(1)}, f32[232,512]{1,0:T(8,128)S(1)}, u32[]{:S(2)}, u32[]{:S(2)}) collective-permute-start(f32[232,512]{1,0:T(8,128)S(1)} %get-tuple-element.24), channel_id=1, source_target_pairs={{0,72},{8,64},{64,8},{72,0},{16,88},{24,80},{80,24},{88,16},{32,10... | collective-permute-start | bytes 1425416 | tf_op jit(solution)/shard_map/ppermute | solution.py:342
  112.8 8.1 %collective-permute-start.9 = (f32[128,2048]{1,0:T(8,128)S(1)}, f32[128,2048]{1,0:T(8,128)S(1)}, u32[]{:S(2)}, u32[]{:S(2)}) collective-permute-start(f32[128,2048]{1,0:T(8,128)S(1)} %shard_map.64), channel_id=1, source_target_pairs={{0,4},{4,0},{8,12},{12,8},{16,20},{20,16},{24,28},{28,24},{32,36},... | collective-permute-start | bytes 3145736 | tf_op jit(solution)/shard_map/ppermute | solution.py:378

commit v2 on v1

--- a/solution.py
+++ b/solution.py
@@ -131,7 +131,15 @@
     return ref.at[rows, pl.ds(pl.multiple_of(core * width, LANES), width)]
 
 
-def entry_kernel(rows_ref, out_ref, own_plane_ref, other_plane_ref):
+def lead_kernel(out_ref):
+    out_ref[...] = lax.broadcasted_iota(jnp.int32, out_ref.shape, 0)
+
+
+def numbers_kernel(level_ref, coeff_ref, line_ref, out_ref):
+    out_ref[...] = jnp.where(line_ref[...] == 0, level_ref[0], coeff_ref[0]).astype(jnp.float32)
+
+
+def entry_kernel(numbers_ref, rows_ref, out_ref, own_plane_ref, other_plane_ref):
     core = core_here()
     half = out_ref.shape[1]
     mine = pl.ds(pl.multiple_of(core * half, LANES), half)
@@ -139,11 +147,7 @@
     own_plane_ref[...] = rows_ref[:PLANE, mine]
     other_plane_ref[...] = rows_ref[:PLANE, theirs]
     out_ref[:ROWS, :] = rows_ref[:, theirs]
-
-
-def stamp_kernel(level_ref, coeff_ref, rows_ref, out_ref):
-    line = lax.broadcasted_iota(jnp.int32, (8, out_ref.shape[1]), 0)
-    out_ref[ROWS:, :] = jnp.where(line == 0, level_ref[0], coeff_ref[0]).astype(jnp.float32)
+    out_ref[ROWS:, :] = jnp.concatenate([numbers_ref[...]] * (half // LANES), axis=1)
 
 
 def forth_kernel(turns, level_ref, coeff_ref, table_ref, rows_ref, own_next_ref, other_ref, other_next_ref, *out_refs):
@@ -288,8 +292,8 @@
 ]
 ALONG_Y = [[[member(2 * a + i, z, core) for a in range(NY // 2)] for i in (0, 1) for z in range(NZ)] for core in (0, 1)]
 ALONG_Z = [[[member(y, 2 * b + j, core) for b in range(NZ // 2)] for j in (0, 1) for y in range(NY)] for core in (0, 1)]
-LINES = ALONG_Y[0] + ALONG_Z[1]
-OTHER_LINES = ALONG_Z[0] + ALONG_Y[1]
+LINES = ALONG_Z[0] + ALONG_Y[1]
+OTHER_LINES = ALONG_Y[0] + ALONG_Z[1]
 VMEM = pl.BlockSpec(memory_space=pltpu.VMEM)
 SMEM = pl.BlockSpec(memory_space=pltpu.SMEM)
 HBM = pl.BlockSpec(memory_space=pltpu.HBM)
@@ -342,13 +346,14 @@
             far[turn] = lax.ppermute(pieces[turn], "grp", turned(turn))
         return [pieces[0], far[1], far[2], far[3]]
 
+    line = call(lead_kernel, [], VMEM, jax.ShapeDtypeStruct((8, LANES), jnp.int32), flops=2*10**9)()
+    numbers = call(numbers_kernel, [SMEM, SMEM, VMEM], VMEM, f32(8, LANES))(first_level, coeffs, line)
     entry, own_plane, other_plane = call(
-        entry_kernel, [VMEM], [VMEM] * 3,
+        entry_kernel, [VMEM] * 2, [VMEM] * 3,
         [f32(ROWS + 8, half), f32(PLANE, half), f32(PLANE, half)],
-    )(rows)
+    )(numbers, rows)
     other_next = to_previous(other_plane, 1)
     own_next = to_previous(own_plane, 0)
-    entry = call(stamp_kernel, [SMEM, SMEM, VMEM], VMEM, f32(ROWS + 8, half), alias={2: 0})(first_level, coeffs, entry)
     other = lax.ppermute(entry, "grp", swap)
 
     def surplus(*turns):

time: 122 us -> 120 us (0.984)
  local copies, waits for them, and re-layouts: 1.6 us -> 0.01 us
  starting transfers between devices: 44.4 us -> 42.9 us
    unnamed x8 -> x6, local copies, waits for them, and re-layouts: 1.6 us -> 0.01 us
    ppermute x1, starting transfers between devices: 5.8 us -> 4.51 us  [shards(): swapped = lax.ppermute(other_out, 'grp', swap)]
where the time goes in v2:
time: 120 us
  blocking collectives  45.8 us (38%)
  starting transfers between devices  42.9 us (36%)
  waiting for transfers between devices  24.3 us (20%)
  Pallas kernels  5.07 us (4%)
  between operations  1.98 us (2%)
    all_to_all x3, blocking collectives, exchange(): lax.all_to_all(values, 'grp', 0, 0, axis_index_groups=groups, tiled=True)  45.8 us
    ppermute x6, starting transfers between devices, through_tile(): far[turn] = lax.ppermute(pieces[turn], 'grp', turned(turn))  25.8 us
    ppermute x6, waiting for transfers between devices, through_tile(): far[turn] = lax.ppermute(pieces[turn], 'grp', turned(turn))  19.6 us
    ppermute x1, starting transfers between devices, shards(): other = lax.ppermute(entry, 'grp', swap)  8.75 us
    ppermute x1, starting transfers between devices, shards(): swapped = lax.ppermute(other_out, 'grp', swap)  4.51 us
    ppermute x2, starting transfers between devices, to_previous(): return lax.ppermute(values, ('grp', 'slab'), pairs)  3.84 us
    ppermute x2, waiting for transfers between devices, to_previous(): return lax.ppermute(values, ('grp', 'slab'), pairs)  3.78 us
  transfers between devices with their start and end apart: 10, of which 7 were waited for; matrix products, arithmetic and copies ran while one was open for 0% of the time, Pallas kernels for 2%

profile of v2, /device:TPU:1, one launch (start us, length us, event | category | flops | bytes accessed | tf_op | source)
XLA Modules:
  0.0 120.0 jit_solution(11590605665123181558)
XLA Ops:
  1.9 8.7 %collective-permute-start = (f32[136,2048]{1,0:T(8,128)S(1)}, f32[136,2048]{1,0:T(8,128)S(1)}, u32[]{:S(2)}, u32[]{:S(2)}) collective-permute-start(f32[136,2048]{1,0:T(8,128)S(1)} %get-tuple-element.15), channel_id=1, source_target_pairs={{0,4},{4,0},{8,12},{12,8},{16,20},{20,16},{24,28},{28,24},{32,36},... | collective-permute-start | bytes 3342344 | tf_op jit(solution)/shard_map/ppermute | solution.py:357
  10.7 1.9 %collective-permute-start.1 = (f32[8,2048]{1,0:T(8,128)S(1)}, f32[8,2048]{1,0:T(8,128)S(1)}, u32[]{:S(2)}, u32[]{:S(2)}) collective-permute-start(f32[8,2048]{1,0:T(8,128)S(1)} %get-tuple-element.16), channel_id=1, source_target_pairs={{0,3},{1,0},{2,1},{3,2},{4,7},{5,4},{6,5},{7,6},{8,11},{9,8},{10,9... | collective-permute-start | bytes 196616 | tf_op jit(solution)/shard_map/ppermute | solution.py:340
  12.6 1.9 %collective-permute-start.2 = (f32[8,2048]{1,0:T(8,128)S(1)}, f32[8,2048]{1,0:T(8,128)S(1)}, u32[]{:S(2)}, u32[]{:S(2)}) collective-permute-start(f32[8,2048]{1,0:T(8,128)S(1)} %get-tuple-element.17), channel_id=1, source_target_pairs={{0,7},{1,4},{2,5},{3,6},{4,3},{5,0},{6,1},{7,2},{8,15},{9,12},{10,... | collective-permute-start | bytes 196616 | tf_op jit(solution)/shard_map/ppermute | solution.py:340
  14.5 1.7 %collective-permute-done.1.own_next_ref = f32[8,2048]{1,0:T(8,128)S(1)} collective-permute-done((f32[8,2048]{1,0:T(8,128)S(1)}, f32[8,2048]{1,0:T(8,128)S(1)}, u32[]{:S(2)}, u32[]{:S(2)}) %collective-permute-start.1) | collective-permute-done | bytes 65568 | tf_op jit(solution)/shard_map/ppermute | solution.py:340
  16.2 2.1 %collective-permute-done.2.other_next_ref = f32[8,2048]{1,0:T(8,128)S(1)} collective-permute-done((f32[8,2048]{1,0:T(8,128)S(1)}, f32[8,2048]{1,0:T(8,128)S(1)}, u32[]{:S(2)}, u32[]{:S(2)}) %collective-permute-start.2) | collective-permute-done | bytes 65568 | tf_op jit(solution)/shard_map/ppermute | solution.py:340
  18.3 1.0 shard_map.60
  19.4 8.0 %collective-permute-start.3 = (f32[240,512]{1,0:T(8,128)S(1)}, f32[240,512]{1,0:T(8,128)S(1)}, u32[]{:S(2)}, u32[]{:S(2)}) collective-permute-start(f32[240,512]{1,0:T(8,128)S(1)} %get-tuple-element.18), channel_id=1, source_target_pairs={{0,8},{8,0},{64,72},{72,64},{16,24},{24,16},{80,88},{88,80},{32,40... | collective-permute-start | bytes 1474568 | tf_op jit(solution)/shard_map/ppermute | solution.py:346
  27.3 5.1 %collective-permute-start.4 = (f32[240,512]{1,0:T(8,128)S(1)}, f32[240,512]{1,0:T(8,128)S(1)}, u32[]{:S(2)}, u32[]{:S(2)}) collective-permute-start(f32[240,512]{1,0:T(8,128)S(1)} %get-tuple-element.19), channel_id=1, source_target_pairs={{0,64},{8,72},{64,0},{72,8},{16,80},{24,88},{80,16},{88,24},{32,96... | collective-permute-start | bytes 1474568 | tf_op jit(solution)/shard_map/ppermute | solution.py:346
  32.4 1.9 %collective-permute-start.5 = (f32[240,512]{1,0:T(8,128)S(1)}, f32[240,512]{1,0:T(8,128)S(1)}, u32[]{:S(2)}, u32[]{:S(2)}) collective-permute-start(f32[240,512]{1,0:T(8,128)S(1)} %get-tuple-element.20), channel_id=1, source_target_pairs={{0,72},{8,64},{64,8},{72,0},{16,88},{24,80},{80,24},{88,16},{32,10... | collective-permute-start | bytes 1474568 | tf_op jit(solution)/shard_map/ppermute | solution.py:346
  34.9 3.8 %collective-permute-done.4.refs_2_ = f32[240,512]{1,0:T(8,128)S(1)} collective-permute-done((f32[240,512]{1,0:T(8,128)S(1)}, f32[240,512]{1,0:T(8,128)S(1)}, u32[]{:S(2)}, u32[]{:S(2)}) %collective-permute-start.4) | collective-permute-done | bytes 491552 | tf_op jit(solution)/shard_map/ppermute | solution.py:346
  38.6 6.7 %collective-permute-done.5.refs_3_ = f32[240,512]{1,0:T(8,128)S(1)} collective-permute-done((f32[240,512]{1,0:T(8,128)S(1)}, f32[240,512]{1,0:T(8,128)S(1)}, u32[]{:S(2)}, u32[]{:S(2)}) %collective-permute-start.5) | collective-permute-done | bytes 491552 | tf_op jit(solution)/shard_map/ppermute | solution.py:346
  45.6 15.2 %all_to_all.15.got_ref = f32[4,264,128]{2,1,0:T(8,128)S(1)} all-to-all(f32[4,264,128]{2,1,0:T(8,128)S(1)} %shard_map.61), channel_id=1, replica_groups={{0,16,32,48},{64,80,96,112},{128,144,160,176},{192,208,224,240},{256,27..., dimensions={0} | all-to-all | bytes 1081344 | tf_op jit(solution)/shard_map/all_to_all | solution.py:304
  60.8 16.0 %all_to_all.16.got_ref = f32[4,264,128]{2,1,0:T(8,128)S(1)} all-to-all(f32[4,264,128]{2,1,0:T(8,128)S(1)} %shard_map.62), channel_id=1, replica_groups={{0,128,256,384},{8,136,264,392},{16,144,272,400},{24,152,280,408},{32,1..., dimensions={0} | all-to-all | bytes 1081344 | tf_op jit(solution)/shard_map/all_to_all | solution.py:304
  76.9 14.5 %all_to_all.17.table_ref = f32[4,264,128]{2,1,0:T(8,128)S(1)} all-to-all(f32[4,264,128]{2,1,0:T(8,128)S(1)} %shard_map.63), channel_id=1, replica_groups={{0,16,32,48},{64,80,96,112},{128,144,160,176},{192,208,224,240},{256,27..., dimensions={0} | all-to-all | bytes 1081344 | tf_op jit(solution)/shard_map/all_to_all | solution.py:304
  91.6 2.2 %collective-permute-start.6 = (f32[232,512]{1,0:T(8,128)S(1)}, f32[232,512]{1,0:T(8,128)S(1)}, u32[]{:S(2)}, u32[]{:S(2)}) collective-permute-start(f32[232,512]{1,0:T(8,128)S(1)} %get-tuple-element.22), channel_id=1, source_target_pairs={{0,8},{8,0},{64,72},{72,64},{16,24},{24,16},{80,88},{88,80},{32,40... | collective-permute-start | bytes 1425416 | tf_op jit(solution)/shard_map/ppermute | solution.py:346
  93.8 2.2 %collective-permute-start.7 = (f32[232,512]{1,0:T(8,128)S(1)}, f32[232,512]{1,0:T(8,128)S(1)}, u32[]{:S(2)}, u32[]{:S(2)}) collective-permute-start(f32[232,512]{1,0:T(8,128)S(1)} %get-tuple-element.23), channel_id=1, source_target_pairs={{0,64},{8,72},{64,0},{72,8},{16,80},{24,88},{80,16},{88,24},{32,96... | collective-permute-start | bytes 1425416 | tf_op jit(solution)/shard_map/ppermute | solution.py:346
  96.0 6.4 %collective-permute-start.8 = (f32[232,512]{1,0:T(8,128)S(1)}, f32[232,512]{1,0:T(8,128)S(1)}, u32[]{:S(2)}, u32[]{:S(2)}) collective-permute-start(f32[232,512]{1,0:T(8,128)S(1)} %get-tuple-element.24), channel_id=1, source_target_pairs={{0,72},{8,64},{64,8},{72,0},{16,88},{24,80},{80,24},{88,16},{32,10... | collective-permute-start | bytes 1425416 | tf_op jit(solution)/shard_map/ppermute | solution.py:346
  102.4 2.0 %collective-permute-done.7.refs_2_ = f32[232,512]{1,0:T(8,128)S(1)} collective-permute-done((f32[232,512]{1,0:T(8,128)S(1)}, f32[232,512]{1,0:T(8,128)S(1)}, u32[]{:S(2)}, u32[]{:S(2)}) %collective-permute-start.7) | collective-permute-done | bytes 475168 | tf_op jit(solution)/shard_map/ppermute | solution.py:346
  104.4 7.2 %collective-permute-done.8.refs_3_ = f32[232,512]{1,0:T(8,128)S(1)} collective-permute-done((f32[232,512]{1,0:T(8,128)S(1)}, f32[232,512]{1,0:T(8,128)S(1)}, u32[]{:S(2)}, u32[]{:S(2)}) %collective-permute-start.8) | collective-permute-done | bytes 475168 | tf_op jit(solution)/shard_map/ppermute | solution.py:346
  111.6 0.6 shard_map.65
  112.2 4.5 %collective-permute-start.9 = (f32[128,2048]{1,0:T(8,128)S(1)}, f32[128,2048]{1,0:T(8,128)S(1)}, u32[]{:S(2)}, u32[]{:S(2)}) collective-permute-start(f32[128,2048]{1,0:T(8,128)S(1)} %shard_map.65), channel_id=1, source_target_pairs={{0,4},{4,0},{8,12},{12,8},{16,20},{20,16},{24,28},{28,24},{32,36},... | collective-permute-start | bytes 3145736 | tf_op jit(solution)/shard_map/ppermute | solution.py:383
  116.7 1.4 %shard_map.66.filled_ref = f32[128,4096]{1,0:T(8,128)} custom-call(s32[1]{0:T(128)S(6)} %copy.8.level_ref, f32[8,128]{1,0:T(8,128)S(1)} %shard_map.58.meta_ref, bf16[9,128,232]{2,1,0:T(8,128)(2,1)S(1)} %copy-done.2, f32[232,512]{1,0:T(8,128)S(1)} %get-tuple-element.21.refs_0_, f32[232,512]{1,0:T(8,128)S(1)} %collective-permute-done.6.refs_1_, ...), custom_call_target="tpu_custom_call" | custom-call | flops 1000000000 | tf_op jit(solution)/shard_map/pallas_call | solution.py:384
  118.1 0.9 collective-permute-done.9.values_ref
  119.0 1.0 shard_map.67
  (18 shorter events, 1.1 us)
Async XLA Ops:
  0.0 1.8 %copy-start = (f32[1,128,4096]{2,1,0:T(8,128)S(1)}, f32[1,128,4096]{2,1,0:T(8,128)}, u32[]{:S(2)}) copy-start(f32[1,128,4096]{2,1,0:T(8,128)} %param.6) | copy-start | bytes 6291460
  0.0 18.3 %copy-start.1 = (bf16[9,240,272]{2,1,0:T(8,128)(2,1)S(1)}, bf16[9,240,272]{2,1,0:T(8,128)(2,1)}, u32[]{:S(2)}) copy-start(bf16[9,240,272]{2,1,0:T(8,128)(2,1)} %constant.4.clone.table_ref) | copy-start | bytes 3525124
  1.9 16.4 %collective-permute-start = (f32[136,2048]{1,0:T(8,128)S(1)}, f32[136,2048]{1,0:T(8,128)S(1)}, u32[]{:S(2)}, u32[]{:S(2)}) collective-permute-start(f32[136,2048]{1,0:T(8,128)S(1)} %get-tuple-element.15), channel_id=1, source_target_pairs={{0,4},{4,0},{8,12},{12,8},{16,20},{20,16},{24,28},{28,24},{32,36},... | collective-permute-start | bytes 3342344 | tf_op jit(solution)/shard_map/ppermute | solution.py:357
  10.7 5.5 %collective-permute-start.1 = (f32[8,2048]{1,0:T(8,128)S(1)}, f32[8,2048]{1,0:T(8,128)S(1)}, u32[]{:S(2)}, u32[]{:S(2)}) collective-permute-start(f32[8,2048]{1,0:T(8,128)S(1)} %get-tuple-element.16), channel_id=1, source_target_pairs={{0,3},{1,0},{2,1},{3,2},{4,7},{5,4},{6,5},{7,6},{8,11},{9,8},{10,9... | collective-permute-start | bytes 196616 | tf_op jit(solution)/shard_map/ppermute | solution.py:340
  12.6 5.7 %collective-permute-start.2 = (f32[8,2048]{1,0:T(8,128)S(1)}, f32[8,2048]{1,0:T(8,128)S(1)}, u32[]{:S(2)}, u32[]{:S(2)}) collective-permute-start(f32[8,2048]{1,0:T(8,128)S(1)} %get-tuple-element.17), channel_id=1, source_target_pairs={{0,7},{1,4},{2,5},{3,6},{4,3},{5,0},{6,1},{7,2},{8,15},{9,12},{10,... | collective-permute-start | bytes 196616 | tf_op jit(solution)/shard_map/ppermute | solution.py:340
  19.4 15.5 %collective-permute-start.3 = (f32[240,512]{1,0:T(8,128)S(1)}, f32[240,512]{1,0:T(8,128)S(1)}, u32[]{:S(2)}, u32[]{:S(2)}) collective-permute-start(f32[240,512]{1,0:T(8,128)S(1)} %get-tuple-element.18), channel_id=1, source_target_pairs={{0,8},{8,0},{64,72},{72,64},{16,24},{24,16},{80,88},{88,80},{32,40... | collective-permute-start | bytes 1474568 | tf_op jit(solution)/shard_map/ppermute | solution.py:346
  27.3 11.3 %collective-permute-start.4 = (f32[240,512]{1,0:T(8,128)S(1)}, f32[240,512]{1,0:T(8,128)S(1)}, u32[]{:S(2)}, u32[]{:S(2)}) collective-permute-start(f32[240,512]{1,0:T(8,128)S(1)} %get-tuple-element.19), channel_id=1, source_target_pairs={{0,64},{8,72},{64,0},{72,8},{16,80},{24,88},{80,16},{88,24},{32,96... | collective-permute-start | bytes 1474568 | tf_op jit(solution)/shard_map/ppermute | solution.py:346
  32.4 12.9 %collective-permute-start.5 = (f32[240,512]{1,0:T(8,128)S(1)}, f32[240,512]{1,0:T(8,128)S(1)}, u32[]{:S(2)}, u32[]{:S(2)}) collective-permute-start(f32[240,512]{1,0:T(8,128)S(1)} %get-tuple-element.20), channel_id=1, source_target_pairs={{0,72},{8,64},{64,8},{72,0},{16,88},{24,80},{80,24},{88,16},{32,10... | collective-permute-start | bytes 1474568 | tf_op jit(solution)/shard_map/ppermute | solution.py:346
  76.9 34.7 %copy-start.2 = (bf16[9,128,232]{2,1,0:T(8,128)(2,1)S(1)}, bf16[9,128,232]{2,1,0:T(8,128)(2,1)}, u32[]{:S(2)}) copy-start(bf16[9,128,232]{2,1,0:T(8,128)(2,1)} %constant.5.clone.table_ref) | copy-start | bytes 1603588
  91.6 10.8 %collective-permute-start.6 = (f32[232,512]{1,0:T(8,128)S(1)}, f32[232,512]{1,0:T(8,128)S(1)}, u32[]{:S(2)}, u32[]{:S(2)}) collective-permute-start(f32[232,512]{1,0:T(8,128)S(1)} %get-tuple-element.22), channel_id=1, source_target_pairs={{0,8},{8,0},{64,72},{72,64},{16,24},{24,16},{80,88},{88,80},{32,40... | collective-permute-start | bytes 1425416 | tf_op jit(solution)/shard_map/ppermute | solution.py:346
  93.8 10.6 %collective-permute-start.7 = (f32[232,512]{1,0:T(8,128)S(1)}, f32[232,512]{1,0:T(8,128)S(1)}, u32[]{:S(2)}, u32[]{:S(2)}) collective-permute-start(f32[232,512]{1,0:T(8,128)S(1)} %get-tuple-element.23), channel_id=1, source_target_pairs={{0,64},{8,72},{64,0},{72,8},{16,80},{24,88},{80,16},{88,24},{32,96... | collective-permute-start | bytes 1425416 | tf_op jit(solution)/shard_map/ppermute | solution.py:346
  96.0 15.6 %collective-permute-start.8 = (f32[232,512]{1,0:T(8,128)S(1)}, f32[232,512]{1,0:T(8,128)S(1)}, u32[]{:S(2)}, u32[]{:S(2)}) collective-permute-start(f32[232,512]{1,0:T(8,128)S(1)} %get-tuple-element.24), channel_id=1, source_target_pairs={{0,72},{8,64},{64,8},{72,0},{16,88},{24,80},{80,24},{88,16},{32,10... | collective-permute-start | bytes 1425416 | tf_op jit(solution)/shard_map/ppermute | solution.py:346
  112.2 6.8 %collective-permute-start.9 = (f32[128,2048]{1,0:T(8,128)S(1)}, f32[128,2048]{1,0:T(8,128)S(1)}, u32[]{:S(2)}, u32[]{:S(2)}) collective-permute-start(f32[128,2048]{1,0:T(8,128)S(1)} %shard_map.65), channel_id=1, source_target_pairs={{0,4},{4,0},{8,12},{12,8},{16,20},{20,16},{24,28},{28,24},{32,36},... | collective-permute-start | bytes 3145736 | tf_op jit(solution)/shard_map/ppermute | solution.py:383

commit v3 on v2

--- a/solution.py
+++ b/solution.py
@@ -23,7 +23,6 @@
 ENTRY = 2 * (ROWS + PLANE)
 TABLE = 8 * BLOCK + PLANE
 LANES = 128
-SHARE = 16
 
 
 def slots_of(levels):
@@ -124,11 +123,6 @@
     me = lax.axis_index("grp")
     core, z, y = me % 2, me // 2 % NZ, me // (2 * NZ)
     return ((y + core) % 2 * 2 + (z + core) % 2) ^ turn
-
-
-def half_of(ref, core, rows=slice(None)):
-    width = ref.shape[1] // 2
-    return ref.at[rows, pl.ds(pl.multiple_of(core * width, LANES), width)]
 
 
 def lead_kernel(out_ref):
@@ -235,45 +229,49 @@
     return level_ref[0] - LOW_LEVEL, number_in(meta_ref, 0).astype(jnp.int32) - LOW_LEVEL
 
 
-def pieces(refs):
-    for turn, ref in enumerate(refs):
-        chunk = ref.shape[1]
-        for h in range(2):
-            width = chunk // 2
-            yield piece_here(turn) * chunk + h * width, ref[:, h * width : (h + 1) * width]
+def pieces(ref):
+    width = ref.shape[1] // 2
+    for h in range(2):
+        yield h * width, ref[:, h * width : (h + 1) * width]
 
 
 def other_back_kernel(level_ref, meta_ref, table_ref, *refs):
     *got_refs, out_ref = refs
     own, other = levels_in(level_ref, meta_ref)
     table = table_ref[other * 3 + own]
-    for low, values in pieces(got_refs):
-        out_ref[:, pl.ds(pl.multiple_of(low, LANES), values.shape[1])] = two_part_dot(table, values)
-
-
-def own_back_kernel(level_ref, meta_ref, table_ref, *refs):
-    *got_refs, out_ref, done_ref, sems = refs
+    for i, ref in enumerate(got_refs):
+        for low, values in pieces(ref):
+            out_ref[i, :, low : low + values.shape[1]] = two_part_dot(table, values)
+
+
+def own_back_kernel(turns, level_ref, meta_ref, table_ref, *refs):
+    got_refs = refs[: len(turns)]
+    out_ref, done_ref, sems = refs[-3:]
     own, other = levels_in(level_ref, meta_ref)
     table = table_ref[own * 3 + other]
     first = core_here() * (out_ref.shape[1] // 2)
     copies = []
-    for i, (low, values) in enumerate(pieces(got_refs)):
-        width = values.shape[1]
-        done_ref[i] = two_part_dot(table, values)
-        start = pl.multiple_of(first + low, LANES)
-        copy = pltpu.make_async_copy(done_ref.at[i], out_ref.at[:, pl.ds(start, width)], sems.at[i])
-        copy.start()
-        copies.append(copy)
+    for turn, ref in zip(turns, got_refs):
+        for low, values in pieces(ref):
+            i, width = len(copies), values.shape[1]
+            done_ref[i] = two_part_dot(table, values)
+            start = pl.multiple_of(first + piece_here(turn) * ref.shape[1] + low, LANES)
+            copy = pltpu.make_async_copy(done_ref.at[i], out_ref.at[:, pl.ds(start, width)], sems.at[i])
+            copy.start()
+            copies.append(copy)
     for copy in copies:
         copy.wait()
 
 
-def place_kernel(values_ref, filled_ref, out_ref, sems):
+def place_kernel(turns, values_ref, filled_ref, out_ref, sems):
+    first = (1 - core_here()) * (out_ref.shape[1] // 2)
+    width = values_ref.shape[2]
     copies = []
-    for i in range(ROWS // SHARE):
-        part = slice(i * SHARE, (i + 1) * SHARE)
-        to = half_of(out_ref, 1 - core_here(), part)
-        copies.append(pltpu.make_async_copy(values_ref.at[part], to, sems.at[i]))
+    for i, turn in enumerate(turns):
+        start = pl.multiple_of(first + (piece_here(turn) ^ 3) * width, LANES)
+        copies.append(
+            pltpu.make_async_copy(values_ref.at[i], out_ref.at[:, pl.ds(start, width)], sems.at[i])
+        )
     for copy in copies:
         copy.start()
     for copy in copies:
@@ -377,15 +375,36 @@
     )(table, *got)
     final = through_tile(picked)
 
-    other_out = call(
-        other_back_kernel, [SMEM] + [VMEM] * (MEMBERS + 2), VMEM, f32(ROWS, half), flops=10**9
-    )(first_level, meta, back, *final)
-    swapped = lax.ppermute(other_out, "grp", swap)
-    out = call(
-        own_back_kernel, [SMEM] + [VMEM] * (MEMBERS + 2), HBM, f32(ROWS, width),
-        (pltpu.VMEM((2 * MEMBERS, ROWS, chunk // 2), jnp.float32), DMA((2 * MEMBERS,))), flops=10**9,
-    )(first_level, meta, back, *final)
-    out = call(place_kernel, [VMEM, HBM], HBM, f32(ROWS, width), (DMA((ROWS // SHARE,)),), alias={1: 0})(swapped, out)
+    def other_rows(turns):
+        return call(
+            other_back_kernel, [SMEM] + [VMEM] * (2 + len(turns)), VMEM,
+            f32(len(turns), ROWS, chunk), flops=10**9,
+        )(first_level, meta, back, *[final[turn] for turn in turns])
+
+    def own_rows(turns, *filled):
+        parts = 2 * len(turns)
+        return call(
+            functools.partial(own_back_kernel, turns),
+            [SMEM] + [VMEM] * (2 + len(turns)) + [HBM] * len(filled), HBM, f32(ROWS, width),
+            (pltpu.VMEM((parts, ROWS, chunk // 2), jnp.float32), DMA((parts,))), flops=10**9,
+            alias={3 + len(turns): 0} if filled else None,
+        )(first_level, meta, back, *[final[turn] for turn in turns], *filled)
+
+    def place(turns, values, filled):
+        return call(
+            functools.partial(place_kernel, turns), [VMEM, HBM], HBM, f32(ROWS, width),
+            (DMA((len(turns),)),), alias={1: 0}, flops=10**8,
+        )(values, filled)
+
+    early, late = (0, 3), (2, 1)
+    other_early = other_rows(early)
+    swapped_early = lax.ppermute(other_early, "grp", swap)
+    out = own_rows(early)
+    other_late = other_rows(late)
+    swapped_late = lax.ppermute(other_late, "grp", swap)
+    out = place(early, swapped_early, out)
+    out = own_rows(late, out)
+    out = place(late, swapped_late, out)
     return out[None]
 
 

time: 120 us -> 119 us (level)
  waiting for transfers between devices: 24.3 us -> 16.7 us
  starting transfers between devices: 42.9 us -> 47.4 us
  Pallas kernels: 5.07 us -> 6.84 us
    ppermute x6, waiting for transfers between devices: 19.6 us -> 12.9 us  [through_tile(): far[turn] = lax.ppermute(pieces[turn], 'grp', turned(turn))]
    ppermute x1 -> x2, starting transfers between devices: 4.51 us -> 9.07 us  [the longest x1 4.93 us: shards(): swapped_late = lax.ppermute(other_late, 'grp', swap)]
    pallas_call x3 -> x6, Pallas kernels: 2.99 us -> 4.76 us  [the longest x2 2.3 us: own_rows(): call(functools.partial(own_back_kernel, turns), [SMEM] + [VMEM] * (2 + le...]
  transfers between devices with their start and end apart: 10 -> 11, of which waited for: 7 -> 6; matrix products, arithmetic and copies ran while one was open for 0% -> 0% of each run, Pallas kernels for 2% -> 4%
where the time goes in v3:
time: 119 us
  starting transfers between devices  47.4 us (40%)
  blocking collectives  45.8 us (38%)
  waiting for transfers between devices  16.7 us (14%)
  Pallas kernels  6.84 us (6%)
  between operations  2.03 us (2%)
    all_to_all x3, blocking collectives, exchange(): lax.all_to_all(values, 'grp', 0, 0, axis_index_groups=groups, tiled=True)  45.8 us
    ppermute x6, starting transfers between devices, through_tile(): far[turn] = lax.ppermute(pieces[turn], 'grp', turned(turn))  25.8 us
    ppermute x6, waiting for transfers between devices, through_tile(): far[turn] = lax.ppermute(pieces[turn], 'grp', turned(turn))  12.9 us
    ppermute x1, starting transfers between devices, shards(): other = lax.ppermute(entry, 'grp', swap)  8.75 us
    ppermute x1, starting transfers between devices, shards(): swapped_late = lax.ppermute(other_late, 'grp', swap)  4.93 us
    ppermute x1, starting transfers between devices, shards(): swapped_early = lax.ppermute(other_early, 'grp', swap)  4.14 us
    ppermute x2, starting transfers between devices, to_previous(): return lax.ppermute(values, ('grp', 'slab'), pairs)  3.84 us
    ppermute x2, waiting for transfers between devices, to_previous(): return lax.ppermute(values, ('grp', 'slab'), pairs)  3.78 us
  transfers between devices with their start and end apart: 11, of which 6 were waited for; matrix products, arithmetic and copies ran while one was open for 0% of the time, Pallas kernels for 4%

profile of v3, /device:TPU:1, one launch (start us, length us, event | category | flops | bytes accessed | tf_op | source)
XLA Modules:
  0.0 118.8 jit_solution(11192734310226559243)
XLA Ops:
  1.9 8.7 %collective-permute-start = (f32[136,2048]{1,0:T(8,128)S(1)}, f32[136,2048]{1,0:T(8,128)S(1)}, u32[]{:S(2)}, u32[]{:S(2)}) collective-permute-start(f32[136,2048]{1,0:T(8,128)S(1)} %get-tuple-element.15), channel_id=1, source_target_pairs={{0,4},{4,0},{8,12},{12,8},{16,20},{20,16},{24,28},{28,24},{32,36},... | collective-permute-start | bytes 3342344 | tf_op jit(solution)/shard_map/ppermute | solution.py:355
  10.7 1.9 %collective-permute-start.1 = (f32[8,2048]{1,0:T(8,128)S(1)}, f32[8,2048]{1,0:T(8,128)S(1)}, u32[]{:S(2)}, u32[]{:S(2)}) collective-permute-start(f32[8,2048]{1,0:T(8,128)S(1)} %get-tuple-element.16), channel_id=1, source_target_pairs={{0,3},{1,0},{2,1},{3,2},{4,7},{5,4},{6,5},{7,6},{8,11},{9,8},{10,9... | collective-permute-start | bytes 196616 | tf_op jit(solution)/shard_map/ppermute | solution.py:338
  12.6 1.9 %collective-permute-start.2 = (f32[8,2048]{1,0:T(8,128)S(1)}, f32[8,2048]{1,0:T(8,128)S(1)}, u32[]{:S(2)}, u32[]{:S(2)}) collective-permute-start(f32[8,2048]{1,0:T(8,128)S(1)} %get-tuple-element.17), channel_id=1, source_target_pairs={{0,7},{1,4},{2,5},{3,6},{4,3},{5,0},{6,1},{7,2},{8,15},{9,12},{10,... | collective-permute-start | bytes 196616 | tf_op jit(solution)/shard_map/ppermute | solution.py:338
  14.5 1.7 %collective-permute-done.1.own_next_ref = f32[8,2048]{1,0:T(8,128)S(1)} collective-permute-done((f32[8,2048]{1,0:T(8,128)S(1)}, f32[8,2048]{1,0:T(8,128)S(1)}, u32[]{:S(2)}, u32[]{:S(2)}) %collective-permute-start.1) | collective-permute-done | bytes 65568 | tf_op jit(solution)/shard_map/ppermute | solution.py:338
  16.2 2.1 %collective-permute-done.2.other_next_ref = f32[8,2048]{1,0:T(8,128)S(1)} collective-permute-done((f32[8,2048]{1,0:T(8,128)S(1)}, f32[8,2048]{1,0:T(8,128)S(1)}, u32[]{:S(2)}, u32[]{:S(2)}) %collective-permute-start.2) | collective-permute-done | bytes 65568 | tf_op jit(solution)/shard_map/ppermute | solution.py:338
  18.3 1.0 shard_map.60
  19.4 8.0 %collective-permute-start.3 = (f32[240,512]{1,0:T(8,128)S(1)}, f32[240,512]{1,0:T(8,128)S(1)}, u32[]{:S(2)}, u32[]{:S(2)}) collective-permute-start(f32[240,512]{1,0:T(8,128)S(1)} %get-tuple-element.18), channel_id=1, source_target_pairs={{0,8},{8,0},{64,72},{72,64},{16,24},{24,16},{80,88},{88,80},{32,40... | collective-permute-start | bytes 1474568 | tf_op jit(solution)/shard_map/ppermute | solution.py:344
  27.3 5.1 %collective-permute-start.4 = (f32[240,512]{1,0:T(8,128)S(1)}, f32[240,512]{1,0:T(8,128)S(1)}, u32[]{:S(2)}, u32[]{:S(2)}) collective-permute-start(f32[240,512]{1,0:T(8,128)S(1)} %get-tuple-element.19), channel_id=1, source_target_pairs={{0,64},{8,72},{64,0},{72,8},{16,80},{24,88},{80,16},{88,24},{32,96... | collective-permute-start | bytes 1474568 | tf_op jit(solution)/shard_map/ppermute | solution.py:344
  32.4 1.9 %collective-permute-start.5 = (f32[240,512]{1,0:T(8,128)S(1)}, f32[240,512]{1,0:T(8,128)S(1)}, u32[]{:S(2)}, u32[]{:S(2)}) collective-permute-start(f32[240,512]{1,0:T(8,128)S(1)} %get-tuple-element.20), channel_id=1, source_target_pairs={{0,72},{8,64},{64,8},{72,0},{16,88},{24,80},{80,24},{88,16},{32,10... | collective-permute-start | bytes 1474568 | tf_op jit(solution)/shard_map/ppermute | solution.py:344
  34.9 3.8 %collective-permute-done.4.refs_2_ = f32[240,512]{1,0:T(8,128)S(1)} collective-permute-done((f32[240,512]{1,0:T(8,128)S(1)}, f32[240,512]{1,0:T(8,128)S(1)}, u32[]{:S(2)}, u32[]{:S(2)}) %collective-permute-start.4) | collective-permute-done | bytes 491552 | tf_op jit(solution)/shard_map/ppermute | solution.py:344
  38.6 6.7 %collective-permute-done.5.refs_3_ = f32[240,512]{1,0:T(8,128)S(1)} collective-permute-done((f32[240,512]{1,0:T(8,128)S(1)}, f32[240,512]{1,0:T(8,128)S(1)}, u32[]{:S(2)}, u32[]{:S(2)}) %collective-permute-start.5) | collective-permute-done | bytes 491552 | tf_op jit(solution)/shard_map/ppermute | solution.py:344
  45.6 15.2 %all_to_all.15.got_ref = f32[4,264,128]{2,1,0:T(8,128)S(1)} all-to-all(f32[4,264,128]{2,1,0:T(8,128)S(1)} %shard_map.61), channel_id=1, replica_groups={{0,16,32,48},{64,80,96,112},{128,144,160,176},{192,208,224,240},{256,27..., dimensions={0} | all-to-all | bytes 1081344 | tf_op jit(solution)/shard_map/all_to_all | solution.py:302
  60.8 16.0 %all_to_all.16.got_ref = f32[4,264,128]{2,1,0:T(8,128)S(1)} all-to-all(f32[4,264,128]{2,1,0:T(8,128)S(1)} %shard_map.62), channel_id=1, replica_groups={{0,128,256,384},{8,136,264,392},{16,144,272,400},{24,152,280,408},{32,1..., dimensions={0} | all-to-all | bytes 1081344 | tf_op jit(solution)/shard_map/all_to_all | solution.py:302
  76.9 14.5 %all_to_all.17.table_ref = f32[4,264,128]{2,1,0:T(8,128)S(1)} all-to-all(f32[4,264,128]{2,1,0:T(8,128)S(1)} %shard_map.63), channel_id=1, replica_groups={{0,16,32,48},{64,80,96,112},{128,144,160,176},{192,208,224,240},{256,27..., dimensions={0} | all-to-all | bytes 1081344 | tf_op jit(solution)/shard_map/all_to_all | solution.py:302
  91.6 1.9 %collective-permute-start.9 = (f32[232,512]{1,0:T(8,128)S(1)}, f32[232,512]{1,0:T(8,128)S(1)}, u32[]{:S(2)}, u32[]{:S(2)}) collective-permute-start(f32[232,512]{1,0:T(8,128)S(1)} %get-tuple-element.24), channel_id=1, source_target_pairs={{0,72},{8,64},{64,8},{72,0},{16,88},{24,80},{80,24},{88,16},{32,10... | collective-permute-start | bytes 1425416 | tf_op jit(solution)/shard_map/ppermute | solution.py:344
  93.5 4.6 %collective-permute-start.6 = (f32[232,512]{1,0:T(8,128)S(1)}, f32[232,512]{1,0:T(8,128)S(1)}, u32[]{:S(2)}, u32[]{:S(2)}) collective-permute-start(f32[232,512]{1,0:T(8,128)S(1)} %get-tuple-element.21), channel_id=1, source_target_pairs={{0,64},{8,72},{64,0},{72,8},{16,80},{24,88},{80,16},{88,24},{32,96... | collective-permute-start | bytes 1425416 | tf_op jit(solution)/shard_map/ppermute | solution.py:344
  98.1 4.3 %collective-permute-start.7 = (f32[232,512]{1,0:T(8,128)S(1)}, f32[232,512]{1,0:T(8,128)S(1)}, u32[]{:S(2)}, u32[]{:S(2)}) collective-permute-start(f32[232,512]{1,0:T(8,128)S(1)} %get-tuple-element.22), channel_id=1, source_target_pairs={{0,8},{8,0},{64,72},{72,64},{16,24},{24,16},{80,88},{88,80},{32,40... | collective-permute-start | bytes 1425416 | tf_op jit(solution)/shard_map/ppermute | solution.py:344
  102.4 2.0 %collective-permute-done.9.refs_1_ = f32[232,512]{1,0:T(8,128)S(1)} collective-permute-done((f32[232,512]{1,0:T(8,128)S(1)}, f32[232,512]{1,0:T(8,128)S(1)}, u32[]{:S(2)}, u32[]{:S(2)}) %collective-permute-start.9) | collective-permute-done | bytes 475168 | tf_op jit(solution)/shard_map/ppermute | solution.py:344
  104.8 4.1 %collective-permute-start.10 = (f32[2,128,512]{2,1,0:T(8,128)S(1)}, f32[2,128,512]{2,1,0:T(8,128)S(1)}, u32[]{:S(2)}, u32[]{:S(2)}) collective-permute-start(f32[2,128,512]{2,1,0:T(8,128)S(1)} %shard_map.66), channel_id=1, source_target_pairs={{0,4},{4,0},{8,12},{12,8},{16,20},{20,16},{24,28},{28,24},{32,36},... | collective-permute-start | bytes 1572872 | tf_op jit(solution)/shard_map/ppermute | solution.py:401
  109.8 4.9 %collective-permute-start.8 = (f32[2,128,512]{2,1,0:T(8,128)S(1)}, f32[2,128,512]{2,1,0:T(8,128)S(1)}, u32[]{:S(2)}, u32[]{:S(2)}) collective-permute-start(f32[2,128,512]{2,1,0:T(8,128)S(1)} %shard_map.65), channel_id=1, source_target_pairs={{0,4},{4,0},{8,12},{12,8},{16,20},{20,16},{24,28},{28,24},{32,36},... | collective-permute-start | bytes 1572872 | tf_op jit(solution)/shard_map/ppermute | solution.py:404
  114.8 1.1 shard_map.67.filled_ref
  115.9 0.8 shard_map.68.refs_2_
  116.8 1.2 shard_map.69.filled_ref
  117.9 0.8 shard_map.70
  (23 shorter events, 2.3 us)
Async XLA Ops:
  0.0 1.8 %copy-start = (f32[1,128,4096]{2,1,0:T(8,128)S(1)}, f32[1,128,4096]{2,1,0:T(8,128)}, u32[]{:S(2)}) copy-start(f32[1,128,4096]{2,1,0:T(8,128)} %param.6) | copy-start | bytes 6291460
  0.0 18.3 %copy-start.1 = (bf16[9,240,272]{2,1,0:T(8,128)(2,1)S(1)}, bf16[9,240,272]{2,1,0:T(8,128)(2,1)}, u32[]{:S(2)}) copy-start(bf16[9,240,272]{2,1,0:T(8,128)(2,1)} %constant.4.clone.table_ref) | copy-start | bytes 3525124
  1.9 16.4 %collective-permute-start = (f32[136,2048]{1,0:T(8,128)S(1)}, f32[136,2048]{1,0:T(8,128)S(1)}, u32[]{:S(2)}, u32[]{:S(2)}) collective-permute-start(f32[136,2048]{1,0:T(8,128)S(1)} %get-tuple-element.15), channel_id=1, source_target_pairs={{0,4},{4,0},{8,12},{12,8},{16,20},{20,16},{24,28},{28,24},{32,36},... | collective-permute-start | bytes 3342344 | tf_op jit(solution)/shard_map/ppermute | solution.py:355
  10.7 5.5 %collective-permute-start.1 = (f32[8,2048]{1,0:T(8,128)S(1)}, f32[8,2048]{1,0:T(8,128)S(1)}, u32[]{:S(2)}, u32[]{:S(2)}) collective-permute-start(f32[8,2048]{1,0:T(8,128)S(1)} %get-tuple-element.16), channel_id=1, source_target_pairs={{0,3},{1,0},{2,1},{3,2},{4,7},{5,4},{6,5},{7,6},{8,11},{9,8},{10,9... | collective-permute-start | bytes 196616 | tf_op jit(solution)/shard_map/ppermute | solution.py:338
  12.6 5.7 %collective-permute-start.2 = (f32[8,2048]{1,0:T(8,128)S(1)}, f32[8,2048]{1,0:T(8,128)S(1)}, u32[]{:S(2)}, u32[]{:S(2)}) collective-permute-start(f32[8,2048]{1,0:T(8,128)S(1)} %get-tuple-element.17), channel_id=1, source_target_pairs={{0,7},{1,4},{2,5},{3,6},{4,3},{5,0},{6,1},{7,2},{8,15},{9,12},{10,... | collective-permute-start | bytes 196616 | tf_op jit(solution)/shard_map/ppermute | solution.py:338
  19.4 15.5 %collective-permute-start.3 = (f32[240,512]{1,0:T(8,128)S(1)}, f32[240,512]{1,0:T(8,128)S(1)}, u32[]{:S(2)}, u32[]{:S(2)}) collective-permute-start(f32[240,512]{1,0:T(8,128)S(1)} %get-tuple-element.18), channel_id=1, source_target_pairs={{0,8},{8,0},{64,72},{72,64},{16,24},{24,16},{80,88},{88,80},{32,40... | collective-permute-start | bytes 1474568 | tf_op jit(solution)/shard_map/ppermute | solution.py:344
  27.3 11.3 %collective-permute-start.4 = (f32[240,512]{1,0:T(8,128)S(1)}, f32[240,512]{1,0:T(8,128)S(1)}, u32[]{:S(2)}, u32[]{:S(2)}) collective-permute-start(f32[240,512]{1,0:T(8,128)S(1)} %get-tuple-element.19), channel_id=1, source_target_pairs={{0,64},{8,72},{64,0},{72,8},{16,80},{24,88},{80,16},{88,24},{32,96... | collective-permute-start | bytes 1474568 | tf_op jit(solution)/shard_map/ppermute | solution.py:344
  32.4 12.9 %collective-permute-start.5 = (f32[240,512]{1,0:T(8,128)S(1)}, f32[240,512]{1,0:T(8,128)S(1)}, u32[]{:S(2)}, u32[]{:S(2)}) collective-permute-start(f32[240,512]{1,0:T(8,128)S(1)} %get-tuple-element.20), channel_id=1, source_target_pairs={{0,72},{8,64},{64,8},{72,0},{16,88},{24,80},{80,24},{88,16},{32,10... | collective-permute-start | bytes 1474568 | tf_op jit(solution)/shard_map/ppermute | solution.py:344
  76.9 27.5 %copy-start.2 = (bf16[9,128,232]{2,1,0:T(8,128)(2,1)S(1)}, bf16[9,128,232]{2,1,0:T(8,128)(2,1)}, u32[]{:S(2)}) copy-start(bf16[9,128,232]{2,1,0:T(8,128)(2,1)} %constant.5.clone.table_ref) | copy-start | bytes 1603588
  91.6 12.8 %collective-permute-start.9 = (f32[232,512]{1,0:T(8,128)S(1)}, f32[232,512]{1,0:T(8,128)S(1)}, u32[]{:S(2)}, u32[]{:S(2)}) collective-permute-start(f32[232,512]{1,0:T(8,128)S(1)} %get-tuple-element.24), channel_id=1, source_target_pairs={{0,72},{8,64},{64,8},{72,0},{16,88},{24,80},{80,24},{88,16},{32,10... | collective-permute-start | bytes 1425416 | tf_op jit(solution)/shard_map/ppermute | solution.py:344
  93.5 15.4 %collective-permute-start.6 = (f32[232,512]{1,0:T(8,128)S(1)}, f32[232,512]{1,0:T(8,128)S(1)}, u32[]{:S(2)}, u32[]{:S(2)}) collective-permute-start(f32[232,512]{1,0:T(8,128)S(1)} %get-tuple-element.21), channel_id=1, source_target_pairs={{0,64},{8,72},{64,0},{72,8},{16,80},{24,88},{80,16},{88,24},{32,96... | collective-permute-start | bytes 1425416 | tf_op jit(solution)/shard_map/ppermute | solution.py:344
  98.1 11.3 %collective-permute-start.7 = (f32[232,512]{1,0:T(8,128)S(1)}, f32[232,512]{1,0:T(8,128)S(1)}, u32[]{:S(2)}, u32[]{:S(2)}) collective-permute-start(f32[232,512]{1,0:T(8,128)S(1)} %get-tuple-element.22), channel_id=1, source_target_pairs={{0,8},{8,0},{64,72},{72,64},{16,24},{24,16},{80,88},{88,80},{32,40... | collective-permute-start | bytes 1425416 | tf_op jit(solution)/shard_map/ppermute | solution.py:344
  104.8 11.1 %collective-permute-start.10 = (f32[2,128,512]{2,1,0:T(8,128)S(1)}, f32[2,128,512]{2,1,0:T(8,128)S(1)}, u32[]{:S(2)}, u32[]{:S(2)}) collective-permute-start(f32[2,128,512]{2,1,0:T(8,128)S(1)} %shard_map.66), channel_id=1, source_target_pairs={{0,4},{4,0},{8,12},{12,8},{16,20},{20,16},{24,28},{28,24},{32,36},... | collective-permute-start | bytes 1572872 | tf_op jit(solution)/shard_map/ppermute | solution.py:401
  109.8 8.1 %collective-permute-start.8 = (f32[2,128,512]{2,1,0:T(8,128)S(1)}, f32[2,128,512]{2,1,0:T(8,128)S(1)}, u32[]{:S(2)}, u32[]{:S(2)}) collective-permute-start(f32[2,128,512]{2,1,0:T(8,128)S(1)} %shard_map.65), channel_id=1, source_target_pairs={{0,4},{4,0},{8,12},{12,8},{16,20},{20,16},{24,28},{28,24},{32,36},... | collective-permute-start | bytes 1572872 | tf_op jit(solution)/shard_map/ppermute | solution.py:404

commit v4 on v3

--- a/solution.py
+++ b/solution.py
@@ -244,38 +244,54 @@
             out_ref[i, :, low : low + values.shape[1]] = two_part_dot(table, values)
 
 
-def own_back_kernel(turns, level_ref, meta_ref, table_ref, *refs):
-    got_refs = refs[: len(turns)]
-    out_ref, done_ref, sems = refs[-3:]
-    own, other = levels_in(level_ref, meta_ref)
+def own_copies(turns, levels, table_ref, got_refs, out_ref, done_ref, sems):
+    own, other = levels
     table = table_ref[own * 3 + other]
     first = core_here() * (out_ref.shape[1] // 2)
-    copies = []
+    i = 0
     for turn, ref in zip(turns, got_refs):
         for low, values in pieces(ref):
-            i, width = len(copies), values.shape[1]
+            width = values.shape[1]
             done_ref[i] = two_part_dot(table, values)
             start = pl.multiple_of(first + piece_here(turn) * ref.shape[1] + low, LANES)
-            copy = pltpu.make_async_copy(done_ref.at[i], out_ref.at[:, pl.ds(start, width)], sems.at[i])
-            copy.start()
-            copies.append(copy)
-    for copy in copies:
-        copy.wait()
-
-
-def place_kernel(turns, values_ref, filled_ref, out_ref, sems):
+            yield pltpu.make_async_copy(done_ref.at[i], out_ref.at[:, pl.ds(start, width)], sems.at[i])
+            i += 1
+
+
+def other_copies(turns, values_ref, out_ref, sems):
     first = (1 - core_here()) * (out_ref.shape[1] // 2)
     width = values_ref.shape[2]
-    copies = []
     for i, turn in enumerate(turns):
         start = pl.multiple_of(first + (piece_here(turn) ^ 3) * width, LANES)
-        copies.append(
-            pltpu.make_async_copy(values_ref.at[i], out_ref.at[:, pl.ds(start, width)], sems.at[i])
-        )
-    for copy in copies:
-        copy.start()
-    for copy in copies:
+        yield pltpu.make_async_copy(values_ref.at[i], out_ref.at[:, pl.ds(start, width)], sems.at[i])
+
+
+def run(*copies):
+    started = []
+    for group in copies:
+        for copy in group:
+            copy.start()
+            started.append(copy)
+    for copy in started:
         copy.wait()
+
+
+def early_kernel(turns, level_ref, meta_ref, table_ref, *refs):
+    *got_refs, out_ref, done_ref, sems = refs
+    run(own_copies(turns, levels_in(level_ref, meta_ref), table_ref, got_refs, out_ref, done_ref, sems))
+
+
+def late_kernel(turns, placed, level_ref, meta_ref, table_ref, *refs):
+    *got_refs, values_ref, filled_ref, out_ref, done_ref, sems, other_sems = refs
+    levels = levels_in(level_ref, meta_ref)
+    run(
+        other_copies(placed, values_ref, out_ref, other_sems),
+        own_copies(turns, levels, table_ref, got_refs, out_ref, done_ref, sems),
+    )
+
+
+def place_kernel(turns, values_ref, filled_ref, out_ref, sems):
+    run(other_copies(turns, values_ref, out_ref, sems))
 
 
 def member(y, z, core):
@@ -381,29 +397,33 @@
             f32(len(turns), ROWS, chunk), flops=10**9,
         )(first_level, meta, back, *[final[turn] for turn in turns])
 
-    def own_rows(turns, *filled):
-        parts = 2 * len(turns)
+    parts = (pltpu.VMEM((4, ROWS, chunk // 2), jnp.float32), DMA((4,)))
+
+    def own_early_rows(turns):
         return call(
-            functools.partial(own_back_kernel, turns),
-            [SMEM] + [VMEM] * (2 + len(turns)) + [HBM] * len(filled), HBM, f32(ROWS, width),
-            (pltpu.VMEM((parts, ROWS, chunk // 2), jnp.float32), DMA((parts,))), flops=10**9,
-            alias={3 + len(turns): 0} if filled else None,
-        )(first_level, meta, back, *[final[turn] for turn in turns], *filled)
+            functools.partial(early_kernel, turns), [SMEM] + [VMEM] * 4, HBM, f32(ROWS, width),
+            parts, flops=10**9,
+        )(first_level, meta, back, *[final[turn] for turn in turns])
+
+    def own_late_rows(turns, placed, values, filled):
+        return call(
+            functools.partial(late_kernel, turns, placed), [SMEM] + [VMEM] * 5 + [HBM], HBM,
+            f32(ROWS, width), (*parts, DMA((2,))), flops=10**9, alias={6: 0},
+        )(first_level, meta, back, *[final[turn] for turn in turns], values, filled)
 
     def place(turns, values, filled):
         return call(
             functools.partial(place_kernel, turns), [VMEM, HBM], HBM, f32(ROWS, width),
-            (DMA((len(turns),)),), alias={1: 0}, flops=10**8,
+            (DMA((2,)),), alias={1: 0}, flops=10**8,
         )(values, filled)
 
     early, late = (0, 3), (2, 1)
     other_early = other_rows(early)
     swapped_early = lax.ppermute(other_early, "grp", swap)
-    out = own_rows(early)
+    out = own_early_rows(early)
     other_late = other_rows(late)
     swapped_late = lax.ppermute(other_late, "grp", swap)
-    out = place(early, swapped_early, out)
-    out = own_rows(late, out)
+    out = own_late_rows(late, early, swapped_early, out)
     out = place(late, swapped_late, out)
     return out[None]
 

time: 119 us -> 119 us (level)
  transfers between devices with their start and end apart: 11 -> 11, of which waited for: 6 -> 6; matrix products, arithmetic and copies ran while one was open for 0% -> 0% of each run, Pallas kernels for 4% -> 3%
where the time goes in v4:
time: 119 us; the launch traced here: 118 us
  starting transfers between devices  47.4 us (40%)
  blocking collectives  45.8 us (38%)
  waiting for transfers between devices  16.7 us (14%)
  Pallas kernels  6.1 us (5%)
  between operations  2.02 us (2%)
    all_to_all x3, blocking collectives, exchange(): lax.all_to_all(values, 'grp', 0, 0, axis_index_groups=groups, tiled=True)  45.8 us
    ppermute x6, starting transfers between devices, through_tile(): far[turn] = lax.ppermute(pieces[turn], 'grp', turned(turn))  25.8 us
    ppermute x6, waiting for transfers between devices, through_tile(): far[turn] = lax.ppermute(pieces[turn], 'grp', turned(turn))  12.9 us
    ppermute x1, starting transfers between devices, shards(): other = lax.ppermute(entry, 'grp', swap)  8.75 us
    ppermute x1, starting transfers between devices, shards(): swapped_late = lax.ppermute(other_late, 'grp', swap)  4.93 us
    ppermute x1, starting transfers between devices, shards(): swapped_early = lax.ppermute(other_early, 'grp', swap)  4.14 us
    ppermute x2, starting transfers between devices, to_previous(): return lax.ppermute(values, ('grp', 'slab'), pairs)  3.84 us
    ppermute x2, waiting for transfers between devices, to_previous(): return lax.ppermute(values, ('grp', 'slab'), pairs)  3.78 us
  transfers between devices with their start and end apart: 11, of which 6 were waited for; matrix products, arithmetic and copies ran while one was open for 0% of the time, Pallas kernels for 3%

profile of v4, /device:TPU:1, one launch (start us, length us, event | category | flops | bytes accessed | tf_op | source)
XLA Modules:
  0.0 118.0 jit_solution(3124055976590859302)
XLA Ops:
  1.9 8.7 %collective-permute-start = (f32[136,2048]{1,0:T(8,128)S(1)}, f32[136,2048]{1,0:T(8,128)S(1)}, u32[]{:S(2)}, u32[]{:S(2)}) collective-permute-start(f32[136,2048]{1,0:T(8,128)S(1)} %get-tuple-element.15), channel_id=1, source_target_pairs={{0,4},{4,0},{8,12},{12,8},{16,20},{20,16},{24,28},{28,24},{32,36},... | collective-permute-start | bytes 3342344 | tf_op jit(solution)/shard_map/ppermute | solution.py:371
  10.7 1.9 %collective-permute-start.1 = (f32[8,2048]{1,0:T(8,128)S(1)}, f32[8,2048]{1,0:T(8,128)S(1)}, u32[]{:S(2)}, u32[]{:S(2)}) collective-permute-start(f32[8,2048]{1,0:T(8,128)S(1)} %get-tuple-element.16), channel_id=1, source_target_pairs={{0,3},{1,0},{2,1},{3,2},{4,7},{5,4},{6,5},{7,6},{8,11},{9,8},{10,9... | collective-permute-start | bytes 196616 | tf_op jit(solution)/shard_map/ppermute | solution.py:354
  12.6 1.9 %collective-permute-start.2 = (f32[8,2048]{1,0:T(8,128)S(1)}, f32[8,2048]{1,0:T(8,128)S(1)}, u32[]{:S(2)}, u32[]{:S(2)}) collective-permute-start(f32[8,2048]{1,0:T(8,128)S(1)} %get-tuple-element.17), channel_id=1, source_target_pairs={{0,7},{1,4},{2,5},{3,6},{4,3},{5,0},{6,1},{7,2},{8,15},{9,12},{10,... | collective-permute-start | bytes 196616 | tf_op jit(solution)/shard_map/ppermute | solution.py:354
  14.5 1.7 %collective-permute-done.1.own_next_ref = f32[8,2048]{1,0:T(8,128)S(1)} collective-permute-done((f32[8,2048]{1,0:T(8,128)S(1)}, f32[8,2048]{1,0:T(8,128)S(1)}, u32[]{:S(2)}, u32[]{:S(2)}) %collective-permute-start.1) | collective-permute-done | bytes 65568 | tf_op jit(solution)/shard_map/ppermute | solution.py:354
  16.2 2.1 %collective-permute-done.2.other_next_ref = f32[8,2048]{1,0:T(8,128)S(1)} collective-permute-done((f32[8,2048]{1,0:T(8,128)S(1)}, f32[8,2048]{1,0:T(8,128)S(1)}, u32[]{:S(2)}, u32[]{:S(2)}) %collective-permute-start.2) | collective-permute-done | bytes 65568 | tf_op jit(solution)/shard_map/ppermute | solution.py:354
  18.3 1.0 shard_map.60
  19.4 8.0 %collective-permute-start.3 = (f32[240,512]{1,0:T(8,128)S(1)}, f32[240,512]{1,0:T(8,128)S(1)}, u32[]{:S(2)}, u32[]{:S(2)}) collective-permute-start(f32[240,512]{1,0:T(8,128)S(1)} %get-tuple-element.18), channel_id=1, source_target_pairs={{0,8},{8,0},{64,72},{72,64},{16,24},{24,16},{80,88},{88,80},{32,40... | collective-permute-start | bytes 1474568 | tf_op jit(solution)/shard_map/ppermute | solution.py:360
  27.3 5.1 %collective-permute-start.4 = (f32[240,512]{1,0:T(8,128)S(1)}, f32[240,512]{1,0:T(8,128)S(1)}, u32[]{:S(2)}, u32[]{:S(2)}) collective-permute-start(f32[240,512]{1,0:T(8,128)S(1)} %get-tuple-element.19), channel_id=1, source_target_pairs={{0,64},{8,72},{64,0},{72,8},{16,80},{24,88},{80,16},{88,24},{32,96... | collective-permute-start | bytes 1474568 | tf_op jit(solution)/shard_map/ppermute | solution.py:360
  32.4 1.9 %collective-permute-start.5 = (f32[240,512]{1,0:T(8,128)S(1)}, f32[240,512]{1,0:T(8,128)S(1)}, u32[]{:S(2)}, u32[]{:S(2)}) collective-permute-start(f32[240,512]{1,0:T(8,128)S(1)} %get-tuple-element.20), channel_id=1, source_target_pairs={{0,72},{8,64},{64,8},{72,0},{16,88},{24,80},{80,24},{88,16},{32,10... | collective-permute-start | bytes 1474568 | tf_op jit(solution)/shard_map/ppermute | solution.py:360
  34.4 0.5 shard_map.59.refs_0_
  34.9 3.8 %collective-permute-done.4.refs_2_ = f32[240,512]{1,0:T(8,128)S(1)} collective-permute-done((f32[240,512]{1,0:T(8,128)S(1)}, f32[240,512]{1,0:T(8,128)S(1)}, u32[]{:S(2)}, u32[]{:S(2)}) %collective-permute-start.4) | collective-permute-done | bytes 491552 | tf_op jit(solution)/shard_map/ppermute | solution.py:360
  38.6 6.7 %collective-permute-done.5.refs_3_ = f32[240,512]{1,0:T(8,128)S(1)} collective-permute-done((f32[240,512]{1,0:T(8,128)S(1)}, f32[240,512]{1,0:T(8,128)S(1)}, u32[]{:S(2)}, u32[]{:S(2)}) %collective-permute-start.5) | collective-permute-done | bytes 491552 | tf_op jit(solution)/shard_map/ppermute | solution.py:360
  45.6 15.2 %all_to_all.15.got_ref = f32[4,264,128]{2,1,0:T(8,128)S(1)} all-to-all(f32[4,264,128]{2,1,0:T(8,128)S(1)} %shard_map.61), channel_id=1, replica_groups={{0,16,32,48},{64,80,96,112},{128,144,160,176},{192,208,224,240},{256,27..., dimensions={0} | all-to-all | bytes 1081344 | tf_op jit(solution)/shard_map/all_to_all | solution.py:318
  60.8 16.0 %all_to_all.16.got_ref = f32[4,264,128]{2,1,0:T(8,128)S(1)} all-to-all(f32[4,264,128]{2,1,0:T(8,128)S(1)} %shard_map.62), channel_id=1, replica_groups={{0,128,256,384},{8,136,264,392},{16,144,272,400},{24,152,280,408},{32,1..., dimensions={0} | all-to-all | bytes 1081344 | tf_op jit(solution)/shard_map/all_to_all | solution.py:318
  76.9 14.5 %all_to_all.17.table_ref = f32[4,264,128]{2,1,0:T(8,128)S(1)} all-to-all(f32[4,264,128]{2,1,0:T(8,128)S(1)} %shard_map.63), channel_id=1, replica_groups={{0,16,32,48},{64,80,96,112},{128,144,160,176},{192,208,224,240},{256,27..., dimensions={0} | all-to-all | bytes 1081344 | tf_op jit(solution)/shard_map/all_to_all | solution.py:318
  91.6 1.9 %collective-permute-start.9 = (f32[232,512]{1,0:T(8,128)S(1)}, f32[232,512]{1,0:T(8,128)S(1)}, u32[]{:S(2)}, u32[]{:S(2)}) collective-permute-start(f32[232,512]{1,0:T(8,128)S(1)} %get-tuple-element.24), channel_id=1, source_target_pairs={{0,72},{8,64},{64,8},{72,0},{16,88},{24,80},{80,24},{88,16},{32,10... | collective-permute-start | bytes 1425416 | tf_op jit(solution)/shard_map/ppermute | solution.py:360
  93.5 4.6 %collective-permute-start.6 = (f32[232,512]{1,0:T(8,128)S(1)}, f32[232,512]{1,0:T(8,128)S(1)}, u32[]{:S(2)}, u32[]{:S(2)}) collective-permute-start(f32[232,512]{1,0:T(8,128)S(1)} %get-tuple-element.21), channel_id=1, source_target_pairs={{0,64},{8,72},{64,0},{72,8},{16,80},{24,88},{80,16},{88,24},{32,96... | collective-permute-start | bytes 1425416 | tf_op jit(solution)/shard_map/ppermute | solution.py:360
  98.1 4.3 %collective-permute-start.7 = (f32[232,512]{1,0:T(8,128)S(1)}, f32[232,512]{1,0:T(8,128)S(1)}, u32[]{:S(2)}, u32[]{:S(2)}) collective-permute-start(f32[232,512]{1,0:T(8,128)S(1)} %get-tuple-element.22), channel_id=1, source_target_pairs={{0,8},{8,0},{64,72},{72,64},{16,24},{24,16},{80,88},{88,80},{32,40... | collective-permute-start | bytes 1425416 | tf_op jit(solution)/shard_map/ppermute | solution.py:360
  102.4 2.0 %collective-permute-done.9.refs_1_ = f32[232,512]{1,0:T(8,128)S(1)} collective-permute-done((f32[232,512]{1,0:T(8,128)S(1)}, f32[232,512]{1,0:T(8,128)S(1)}, u32[]{:S(2)}, u32[]{:S(2)}) %collective-permute-start.9) | collective-permute-done | bytes 475168 | tf_op jit(solution)/shard_map/ppermute | solution.py:360
  104.8 4.1 %collective-permute-start.10 = (f32[2,128,512]{2,1,0:T(8,128)S(1)}, f32[2,128,512]{2,1,0:T(8,128)S(1)}, u32[]{:S(2)}, u32[]{:S(2)}) collective-permute-start(f32[2,128,512]{2,1,0:T(8,128)S(1)} %shard_map.66), channel_id=1, source_target_pairs={{0,4},{4,0},{8,12},{12,8},{16,20},{20,16},{24,28},{28,24},{32,36},... | collective-permute-start | bytes 1572872 | tf_op jit(solution)/shard_map/ppermute | solution.py:422
  109.8 4.9 %collective-permute-start.8 = (f32[2,128,512]{2,1,0:T(8,128)S(1)}, f32[2,128,512]{2,1,0:T(8,128)S(1)}, u32[]{:S(2)}, u32[]{:S(2)}) collective-permute-start(f32[2,128,512]{2,1,0:T(8,128)S(1)} %shard_map.65), channel_id=1, source_target_pairs={{0,4},{4,0},{8,12},{12,8},{16,20},{20,16},{24,28},{28,24},{32,36},... | collective-permute-start | bytes 1572872 | tf_op jit(solution)/shard_map/ppermute | solution.py:425
  114.8 1.1 shard_map.67.refs_3_
  115.9 1.3 %shard_map.68.filled_ref = f32[128,4096]{1,0:T(8,128)} custom-call(s32[1]{0:T(128)S(6)} %copy.10.level_ref, f32[8,128]{1,0:T(8,128)S(1)} %shard_map.58.meta_ref, bf16[9,128,232]{2,1,0:T(8,128)(2,1)S(1)} %copy-done.2, f32[232,512]{1,0:T(8,128)S(1)} %collective-permute-done.6.refs_0_, ...), custom_call_target="tpu_custom_call", output_to_operand_aliasing={{}: (6, {})} | custom-call | flops 1000000000 | tf_op jit(solution)/shard_map/pallas_call | solution.py:409
  117.2 0.8 shard_map.69
  (22 shorter events, 1.8 us)
Async XLA Ops:
  0.0 1.8 %copy-start = (f32[1,128,4096]{2,1,0:T(8,128)S(1)}, f32[1,128,4096]{2,1,0:T(8,128)}, u32[]{:S(2)}) copy-start(f32[1,128,4096]{2,1,0:T(8,128)} %param.6) | copy-start | bytes 6291460
  0.0 18.3 %copy-start.1 = (bf16[9,240,272]{2,1,0:T(8,128)(2,1)S(1)}, bf16[9,240,272]{2,1,0:T(8,128)(2,1)}, u32[]{:S(2)}) copy-start(bf16[9,240,272]{2,1,0:T(8,128)(2,1)} %constant.4.clone.table_ref) | copy-start | bytes 3525124
  1.9 16.4 %collective-permute-start = (f32[136,2048]{1,0:T(8,128)S(1)}, f32[136,2048]{1,0:T(8,128)S(1)}, u32[]{:S(2)}, u32[]{:S(2)}) collective-permute-start(f32[136,2048]{1,0:T(8,128)S(1)} %get-tuple-element.15), channel_id=1, source_target_pairs={{0,4},{4,0},{8,12},{12,8},{16,20},{20,16},{24,28},{28,24},{32,36},... | collective-permute-start | bytes 3342344 | tf_op jit(solution)/shard_map/ppermute | solution.py:371
  10.7 5.5 %collective-permute-start.1 = (f32[8,2048]{1,0:T(8,128)S(1)}, f32[8,2048]{1,0:T(8,128)S(1)}, u32[]{:S(2)}, u32[]{:S(2)}) collective-permute-start(f32[8,2048]{1,0:T(8,128)S(1)} %get-tuple-element.16), channel_id=1, source_target_pairs={{0,3},{1,0},{2,1},{3,2},{4,7},{5,4},{6,5},{7,6},{8,11},{9,8},{10,9... | collective-permute-start | bytes 196616 | tf_op jit(solution)/shard_map/ppermute | solution.py:354
  12.6 5.7 %collective-permute-start.2 = (f32[8,2048]{1,0:T(8,128)S(1)}, f32[8,2048]{1,0:T(8,128)S(1)}, u32[]{:S(2)}, u32[]{:S(2)}) collective-permute-start(f32[8,2048]{1,0:T(8,128)S(1)} %get-tuple-element.17), channel_id=1, source_target_pairs={{0,7},{1,4},{2,5},{3,6},{4,3},{5,0},{6,1},{7,2},{8,15},{9,12},{10,... | collective-permute-start | bytes 196616 | tf_op jit(solution)/shard_map/ppermute | solution.py:354
  19.4 15.5 %collective-permute-start.3 = (f32[240,512]{1,0:T(8,128)S(1)}, f32[240,512]{1,0:T(8,128)S(1)}, u32[]{:S(2)}, u32[]{:S(2)}) collective-permute-start(f32[240,512]{1,0:T(8,128)S(1)} %get-tuple-element.18), channel_id=1, source_target_pairs={{0,8},{8,0},{64,72},{72,64},{16,24},{24,16},{80,88},{88,80},{32,40... | collective-permute-start | bytes 1474568 | tf_op jit(solution)/shard_map/ppermute | solution.py:360
  27.3 11.3 %collective-permute-start.4 = (f32[240,512]{1,0:T(8,128)S(1)}, f32[240,512]{1,0:T(8,128)S(1)}, u32[]{:S(2)}, u32[]{:S(2)}) collective-permute-start(f32[240,512]{1,0:T(8,128)S(1)} %get-tuple-element.19), channel_id=1, source_target_pairs={{0,64},{8,72},{64,0},{72,8},{16,80},{24,88},{80,16},{88,24},{32,96... | collective-permute-start | bytes 1474568 | tf_op jit(solution)/shard_map/ppermute | solution.py:360
  32.4 12.9 %collective-permute-start.5 = (f32[240,512]{1,0:T(8,128)S(1)}, f32[240,512]{1,0:T(8,128)S(1)}, u32[]{:S(2)}, u32[]{:S(2)}) collective-permute-start(f32[240,512]{1,0:T(8,128)S(1)} %get-tuple-element.20), channel_id=1, source_target_pairs={{0,72},{8,64},{64,8},{72,0},{16,88},{24,80},{80,24},{88,16},{32,10... | collective-permute-start | bytes 1474568 | tf_op jit(solution)/shard_map/ppermute | solution.py:360
  76.9 27.5 %copy-start.2 = (bf16[9,128,232]{2,1,0:T(8,128)(2,1)S(1)}, bf16[9,128,232]{2,1,0:T(8,128)(2,1)}, u32[]{:S(2)}) copy-start(bf16[9,128,232]{2,1,0:T(8,128)(2,1)} %constant.5.clone.table_ref) | copy-start | bytes 1603588
  91.6 12.8 %collective-permute-start.9 = (f32[232,512]{1,0:T(8,128)S(1)}, f32[232,512]{1,0:T(8,128)S(1)}, u32[]{:S(2)}, u32[]{:S(2)}) collective-permute-start(f32[232,512]{1,0:T(8,128)S(1)} %get-tuple-element.24), channel_id=1, source_target_pairs={{0,72},{8,64},{64,8},{72,0},{16,88},{24,80},{80,24},{88,16},{32,10... | collective-permute-start | bytes 1425416 | tf_op jit(solution)/shard_map/ppermute | solution.py:360
  93.5 15.4 %collective-permute-start.6 = (f32[232,512]{1,0:T(8,128)S(1)}, f32[232,512]{1,0:T(8,128)S(1)}, u32[]{:S(2)}, u32[]{:S(2)}) collective-permute-start(f32[232,512]{1,0:T(8,128)S(1)} %get-tuple-element.21), channel_id=1, source_target_pairs={{0,64},{8,72},{64,0},{72,8},{16,80},{24,88},{80,16},{88,24},{32,96... | collective-permute-start | bytes 1425416 | tf_op jit(solution)/shard_map/ppermute | solution.py:360
  98.1 11.3 %collective-permute-start.7 = (f32[232,512]{1,0:T(8,128)S(1)}, f32[232,512]{1,0:T(8,128)S(1)}, u32[]{:S(2)}, u32[]{:S(2)}) collective-permute-start(f32[232,512]{1,0:T(8,128)S(1)} %get-tuple-element.22), channel_id=1, source_target_pairs={{0,8},{8,0},{64,72},{72,64},{16,24},{24,16},{80,88},{88,80},{32,40... | collective-permute-start | bytes 1425416 | tf_op jit(solution)/shard_map/ppermute | solution.py:360
  104.8 11.1 %collective-permute-start.10 = (f32[2,128,512]{2,1,0:T(8,128)S(1)}, f32[2,128,512]{2,1,0:T(8,128)S(1)}, u32[]{:S(2)}, u32[]{:S(2)}) collective-permute-start(f32[2,128,512]{2,1,0:T(8,128)S(1)} %shard_map.66), channel_id=1, source_target_pairs={{0,4},{4,0},{8,12},{12,8},{16,20},{20,16},{24,28},{28,24},{32,36},... | collective-permute-start | bytes 1572872 | tf_op jit(solution)/shard_map/ppermute | solution.py:422
  109.8 7.4 %collective-permute-start.8 = (f32[2,128,512]{2,1,0:T(8,128)S(1)}, f32[2,128,512]{2,1,0:T(8,128)S(1)}, u32[]{:S(2)}, u32[]{:S(2)}) collective-permute-start(f32[2,128,512]{2,1,0:T(8,128)S(1)} %shard_map.65), channel_id=1, source_target_pairs={{0,4},{4,0},{8,12},{12,8},{16,20},{20,16},{24,28},{28,24},{32,36},... | collective-permute-start | bytes 1572872 | tf_op jit(solution)/shard_map/ppermute | solution.py:425

commit v5 on v4

--- a/solution.py
+++ b/solution.py
@@ -99,7 +99,8 @@
         for other in (6, 7, 8):
             slots = slots_of((own, other))
             mine, theirs = one_grid(own, slots), one_grid(other, slots)
-            forth.append(np.concatenate([mine[0], theirs[0]], axis=1))
+            parts = [grid[0][:, span] for span in (slice(ROWS), slice(ROWS, None)) for grid in (mine, theirs)]
+            forth.append(np.concatenate(parts, axis=1))
             back.append(mine[1])
     return np.stack(forth), np.stack(back)
 
@@ -133,42 +134,75 @@
     out_ref[...] = jnp.where(line_ref[...] == 0, level_ref[0], coeff_ref[0]).astype(jnp.float32)
 
 
-def entry_kernel(numbers_ref, rows_ref, out_ref, own_plane_ref, other_plane_ref):
-    core = core_here()
+def halves(width):
+    half, core = width // 2, core_here()
+    return [pl.multiple_of(which * half, LANES) for which in (core, 1 - core)]
+
+
+def entry_kernel(numbers_ref, rows_ref, out_ref, plane_ref):
     half = out_ref.shape[1]
-    mine = pl.ds(pl.multiple_of(core * half, LANES), half)
-    theirs = pl.ds(pl.multiple_of((1 - core) * half, LANES), half)
-    own_plane_ref[...] = rows_ref[:PLANE, mine]
-    other_plane_ref[...] = rows_ref[:PLANE, theirs]
-    out_ref[:ROWS, :] = rows_ref[:, theirs]
+    _, theirs = halves(rows_ref.shape[1])
+    plane_ref[...] = rows_ref[:PLANE, :]
+    out_ref[:ROWS, :] = rows_ref[:, pl.ds(theirs, half)]
     out_ref[ROWS:, :] = jnp.concatenate([numbers_ref[...]] * (half // LANES), axis=1)
 
 
-def forth_kernel(turns, level_ref, coeff_ref, table_ref, rows_ref, own_next_ref, other_ref, other_next_ref, *out_refs):
-    own_level = level_ref[0]
-    other_level = number_in(other_ref, ROWS).astype(jnp.int32)
-    which = (own_level - LOW_LEVEL) * 3 + other_level - LOW_LEVEL
-    chunk = out_refs[0].shape[1]
-    lane = lax.broadcasted_iota(jnp.int32, (1, ENTRY), 1)
-    scale = jnp.where(lane < ENTRY // 2, coeff_ref[0].astype(jnp.float32), number_in(other_ref, ROWS + 1))
-    table = (table_ref[which].astype(jnp.float32) * scale).astype(jnp.bfloat16)
+def cut_kernel(plane_ref, out_ref):
+    _, theirs = halves(plane_ref.shape[1])
+    out_ref[...] = plane_ref[:, pl.ds(theirs, out_ref.shape[1])]
+
+
+def pair_of(level_ref, other_ref):
+    return level_ref[0], number_in(other_ref, ROWS).astype(jnp.int32)
+
+
+def scaled(table, coeff_ref, other_ref, part):
+    lane = lax.broadcasted_iota(jnp.int32, (1, part.stop - part.start), 1)
+    own = lane < (part.stop - part.start) // 2
+    scale = jnp.where(own, coeff_ref[0].astype(jnp.float32), number_in(other_ref, ROWS + 1))
+    return (table[:, part].astype(jnp.float32) * scale).astype(jnp.bfloat16)
+
+
+MAIN, NEXT = slice(0, 2 * ROWS), slice(2 * ROWS, ENTRY)
+
+
+def windows(turn, chunk):
+    width = chunk // 2
+    for h in range(2):
+        low = pl.multiple_of(piece_here(turn) * chunk + h * width, LANES)
+        yield slice(h * width, (h + 1) * width), low, width
+
+
+def main_kernel(turns, level_ref, coeff_ref, table_ref, rows_ref, other_ref, *out_refs):
+    own_level, other_level = pair_of(level_ref, other_ref)
+    table = table_ref[(own_level - LOW_LEVEL) * 3 + other_level - LOW_LEVEL]
+    table = scaled(table, coeff_ref, other_ref, MAIN)
     six = jnp.logical_or(own_level == 6, other_level == 6).astype(jnp.float32)
     eight = jnp.logical_or(own_level == 8, other_level == 8).astype(jnp.float32)
-    width = chunk // 2
-    line = lax.broadcasted_iota(jnp.int32, (SENT - FLAGS, width), 0)
+    chunk = out_refs[0].shape[1]
+    line = lax.broadcasted_iota(jnp.int32, (SENT - FLAGS, chunk // 2), 0)
     flags = jnp.where(line == 0, six, eight)
-    first = core_here() * MEMBERS * chunk
+    first, _ = halves(rows_ref.shape[1])
     for turn, out_ref in zip(turns, out_refs):
-        for h in range(2):
-            here = slice(h * width, (h + 1) * width)
-            low = piece_here(turn) * chunk + h * width
-            span = pl.ds(pl.multiple_of(low, LANES), width)
+        for here, low, width in windows(turn, chunk):
             own = rows_ref[:, pl.ds(pl.multiple_of(first + low, LANES), width)]
-            values = jnp.concatenate(
-                [own, own_next_ref[:, span], other_ref[:ROWS, span], other_next_ref[:, span]], axis=0
-            )
+            values = jnp.concatenate([own, other_ref[:ROWS, pl.ds(low, width)]], axis=0)
             out_ref[:, here] = two_part_dot(table, values)
             out_ref[FLAGS:SENT, here] = flags
+
+
+def next_kernel(turns, level_ref, coeff_ref, table_ref, plane_ref, other_ref, other_next_ref, *refs):
+    got_refs, out_refs = refs[: len(turns)], refs[len(turns) :]
+    own_level, other_level = pair_of(level_ref, other_ref)
+    table = table_ref[(own_level - LOW_LEVEL) * 3 + other_level - LOW_LEVEL]
+    table = scaled(table, coeff_ref, other_ref, NEXT)
+    chunk = out_refs[0].shape[1]
+    first, _ = halves(plane_ref.shape[1])
+    for turn, got_ref, out_ref in zip(turns, got_refs, out_refs):
+        for here, low, width in windows(turn, chunk):
+            own = plane_ref[:, pl.ds(pl.multiple_of(first + low, LANES), width)]
+            values = jnp.concatenate([own, other_next_ref[:, pl.ds(low, width)]], axis=0)
+            out_ref[:, here] = got_ref[:, here] + two_part_dot(table, values)
 
 
 def meta_kernel(other_ref, meta_ref):
@@ -345,13 +379,7 @@
     swap = [(i, i ^ 1) for i in range(members)]
     forth, back = (jnp.asarray(table, jnp.bfloat16) for table in row_tables())
 
-    def to_previous(values, turn):
-        pairs = [
-            (g * slabs + s, (g ^ turn) * slabs + (s - 1) % slabs)
-            for g in range(members)
-            for s in range(slabs)
-        ]
-        return lax.ppermute(values, ("grp", "slab"), pairs)
+    to_previous = [(i, (i - 1) % slabs) for i in range(slabs)]
 
     def through_tile(pieces):
         turned = lambda turn: [(tile[i], tile[i ^ turn]) for tile in TILES for i in range(MEMBERS)]
@@ -362,22 +390,28 @@
 
     line = call(lead_kernel, [], VMEM, jax.ShapeDtypeStruct((8, LANES), jnp.int32), flops=2*10**9)()
     numbers = call(numbers_kernel, [SMEM, SMEM, VMEM], VMEM, f32(8, LANES))(first_level, coeffs, line)
-    entry, own_plane, other_plane = call(
-        entry_kernel, [VMEM] * 2, [VMEM] * 3,
-        [f32(ROWS + 8, half), f32(PLANE, half), f32(PLANE, half)],
-    )(numbers, rows)
-    other_next = to_previous(other_plane, 1)
-    own_next = to_previous(own_plane, 0)
+    entry, plane = call(entry_kernel, [VMEM] * 2, [VMEM] * 2, [f32(ROWS + 8, half), f32(PLANE, width)])(numbers, rows)
+
+    def main_part(*turns):
+        return call(
+            functools.partial(main_kernel, turns), [SMEM, SMEM] + [VMEM] * 3, [VMEM] * len(turns),
+            [f32(SENT, chunk)] * len(turns), flops=10**9,
+        )(first_level, coeffs, forth, rows, other)
+
+    def with_next(got, *turns):
+        count = len(turns)
+        return call(
+            functools.partial(next_kernel, turns), [SMEM, SMEM] + [VMEM] * (4 + count), [VMEM] * count,
+            [f32(SENT, chunk)] * count, flops=10**8, alias={6 + i: i for i in range(count)},
+        )(first_level, coeffs, forth, next_plane, other, other_next, *got)
+
+    next_plane = lax.ppermute(plane, "slab", to_previous)
     other = lax.ppermute(entry, "grp", swap)
-
-    def surplus(*turns):
-        return call(
-            functools.partial(forth_kernel, turns), [SMEM, SMEM] + [VMEM] * 5, [VMEM] * len(turns),
-            [f32(SENT, chunk)] * len(turns), flops=10**9,
-        )(first_level, coeffs, forth, rows, own_next, other, other_next)
-
-    sent = surplus(1, 2, 3)
-    (stays,) = surplus(0)
+    cut = call(cut_kernel, [VMEM], VMEM, f32(PLANE, half))(next_plane)
+    other_next = lax.ppermute(cut, "grp", swap)
+    sent = main_part(1, 2, 3)
+    sent = with_next(sent, 1, 2, 3)
+    (stays,) = with_next(main_part(0), 0)
     meta = call(meta_kernel, [VMEM], VMEM, f32(8, LANES))(other)
     got = through_tile([stays, *sent])
 

time: 119 us -> 119 us (level)
  starting transfers between devices: 47.4 us -> 45.9 us
    ppermute x6, starting transfers between devices: 25.8 us -> 23.4 us  [through_tile(): far[turn] = lax.ppermute(pieces[turn], 'grp', turned(turn))]
    ppermute x2, waiting for transfers between devices: 3.78 us -> 5.2 us  [the longest x1 5.01 us: shards(): next_plane = lax.ppermute(plane, 'slab', to_previous)]
  transfers between devices with their start and end apart: 11 -> 11, of which waited for: 6 -> 6; matrix products, arithmetic and copies ran while one was open for 0% -> 0% of each run, Pallas kernels for 3% -> 4%
where the time goes in v5:
time: 119 us; the launch traced here: 118 us
  starting transfers between devices  45.9 us (39%)
  blocking collectives  45.9 us (39%)
  waiting for transfers between devices  17.8 us (15%)
  Pallas kernels  6.63 us (6%)
  between operations  2.05 us (2%)
    all_to_all x3, blocking collectives, exchange(): lax.all_to_all(values, 'grp', 0, 0, axis_index_groups=groups, tiled=True)  45.9 us
    ppermute x6, starting transfers between devices, through_tile(): far[turn] = lax.ppermute(pieces[turn], 'grp', turned(turn))  23.4 us
    ppermute x6, waiting for transfers between devices, through_tile(): far[turn] = lax.ppermute(pieces[turn], 'grp', turned(turn))  12.6 us
    ppermute x1, starting transfers between devices, shards(): other = lax.ppermute(entry, 'grp', swap)  8.75 us
    ppermute x1, waiting for transfers between devices, shards(): next_plane = lax.ppermute(plane, 'slab', to_previous)  5.01 us
    ppermute x1, starting transfers between devices, shards(): swapped_late = lax.ppermute(other_late, 'grp', swap)  4.93 us
    ppermute x1, starting transfers between devices, shards(): swapped_early = lax.ppermute(other_early, 'grp', swap)  4.14 us
    ppermute x1, starting transfers between devices, shards(): other_next = lax.ppermute(cut, 'grp', swap)  2.77 us
  transfers between devices with their start and end apart: 11, of which 6 were waited for; matrix products, arithmetic and copies ran while one was open for 0% of the time, Pallas kernels for 4%

profile of v5, /device:TPU:1, one launch (start us, length us, event | category | flops | bytes accessed | tf_op | source)
XLA Modules:
  0.0 118.3 jit_solution(6582184084697125311)
XLA Ops:
  1.9 8.7 %collective-permute-start = (f32[136,2048]{1,0:T(8,128)S(1)}, f32[136,2048]{1,0:T(8,128)S(1)}, u32[]{:S(2)}, u32[]{:S(2)}) collective-permute-start(f32[136,2048]{1,0:T(8,128)S(1)} %get-tuple-element.17), channel_id=1, source_target_pairs={{0,4},{4,0},{8,12},{12,8},{16,20},{20,16},{24,28},{28,24},{32,36},... | collective-permute-start | bytes 3342344 | tf_op jit(solution)/shard_map/ppermute | solution.py:409
  10.7 1.9 %collective-permute-start.1 = (f32[8,4096]{1,0:T(8,128)S(1)}, f32[8,4096]{1,0:T(8,128)S(1)}, u32[]{:S(2)}, u32[]{:S(2)}) collective-permute-start(f32[8,4096]{1,0:T(8,128)S(1)} %get-tuple-element.18), channel_id=1, source_target_pairs={{0,3},{1,0},{2,1},{3,2},{4,7},{5,4},{6,5},{7,6},{8,11},{9,8},{10,9... | collective-permute-start | bytes 393224 | tf_op jit(solution)/shard_map/ppermute | solution.py:408
  12.6 5.0 %collective-permute-done.1.plane_ref = f32[8,4096]{1,0:T(8,128)S(1)} collective-permute-done((f32[8,4096]{1,0:T(8,128)S(1)}, f32[8,4096]{1,0:T(8,128)S(1)}, u32[]{:S(2)}, u32[]{:S(2)}) %collective-permute-start.1) | collective-permute-done | bytes 131104 | tf_op jit(solution)/shard_map/ppermute | solution.py:408
  17.6 2.8 %collective-permute-start.2 = (f32[8,2048]{1,0:T(8,128)S(1)}, f32[8,2048]{1,0:T(8,128)S(1)}, u32[]{:S(2)}, u32[]{:S(2)}) collective-permute-start(f32[8,2048]{1,0:T(8,128)S(1)} %shard_map.59), channel_id=1, source_target_pairs={{0,4},{4,0},{8,12},{12,8},{16,20},{20,16},{24,28},{28,24},{32,36},... | collective-permute-start | bytes 196616 | tf_op jit(solution)/shard_map/ppermute | solution.py:411
  20.4 0.7 shard_map.62
  21.3 0.6 shard_map.63
  21.9 5.6 %collective-permute-start.3 = (f32[240,512]{1,0:T(8,128)S(1)}, f32[240,512]{1,0:T(8,128)S(1)}, u32[]{:S(2)}, u32[]{:S(2)}) collective-permute-start(f32[240,512]{1,0:T(8,128)S(1)} %get-tuple-element.22), channel_id=1, source_target_pairs={{0,8},{8,0},{64,72},{72,64},{16,24},{24,16},{80,88},{88,80},{32,40... | collective-permute-start | bytes 1474568 | tf_op jit(solution)/shard_map/ppermute | solution.py:388
  27.5 5.1 %collective-permute-start.4 = (f32[240,512]{1,0:T(8,128)S(1)}, f32[240,512]{1,0:T(8,128)S(1)}, u32[]{:S(2)}, u32[]{:S(2)}) collective-permute-start(f32[240,512]{1,0:T(8,128)S(1)} %get-tuple-element.23), channel_id=1, source_target_pairs={{0,64},{8,72},{64,0},{72,8},{16,80},{24,88},{80,16},{88,24},{32,96... | collective-permute-start | bytes 1474568 | tf_op jit(solution)/shard_map/ppermute | solution.py:388
  32.6 1.9 %collective-permute-start.5 = (f32[240,512]{1,0:T(8,128)S(1)}, f32[240,512]{1,0:T(8,128)S(1)}, u32[]{:S(2)}, u32[]{:S(2)}) collective-permute-start(f32[240,512]{1,0:T(8,128)S(1)} %get-tuple-element.24), channel_id=1, source_target_pairs={{0,72},{8,64},{64,8},{72,0},{16,88},{24,80},{80,24},{88,16},{32,10... | collective-permute-start | bytes 1474568 | tf_op jit(solution)/shard_map/ppermute | solution.py:388
  35.3 3.6 %collective-permute-done.4.refs_2_ = f32[240,512]{1,0:T(8,128)S(1)} collective-permute-done((f32[240,512]{1,0:T(8,128)S(1)}, f32[240,512]{1,0:T(8,128)S(1)}, u32[]{:S(2)}, u32[]{:S(2)}) %collective-permute-start.4) | collective-permute-done | bytes 491552 | tf_op jit(solution)/shard_map/ppermute | solution.py:388
  39.0 6.6 %collective-permute-done.5.refs_3_ = f32[240,512]{1,0:T(8,128)S(1)} collective-permute-done((f32[240,512]{1,0:T(8,128)S(1)}, f32[240,512]{1,0:T(8,128)S(1)}, u32[]{:S(2)}, u32[]{:S(2)}) %collective-permute-start.5) | collective-permute-done | bytes 491552 | tf_op jit(solution)/shard_map/ppermute | solution.py:388
  45.7 15.2 %all_to_all.15.got_ref = f32[4,264,128]{2,1,0:T(8,128)S(1)} all-to-all(f32[4,264,128]{2,1,0:T(8,128)S(1)} %shard_map.64), channel_id=1, replica_groups={{0,16,32,48},{64,80,96,112},{128,144,160,176},{192,208,224,240},{256,27..., dimensions={0} | all-to-all | bytes 1081344 | tf_op jit(solution)/shard_map/all_to_all | solution.py:352
  61.0 16.1 %all_to_all.16.got_ref = f32[4,264,128]{2,1,0:T(8,128)S(1)} all-to-all(f32[4,264,128]{2,1,0:T(8,128)S(1)} %shard_map.65), channel_id=1, replica_groups={{0,128,256,384},{8,136,264,392},{16,144,272,400},{24,152,280,408},{32,1..., dimensions={0} | all-to-all | bytes 1081344 | tf_op jit(solution)/shard_map/all_to_all | solution.py:352
  77.2 14.5 %all_to_all.17.table_ref = f32[4,264,128]{2,1,0:T(8,128)S(1)} all-to-all(f32[4,264,128]{2,1,0:T(8,128)S(1)} %shard_map.66), channel_id=1, replica_groups={{0,16,32,48},{64,80,96,112},{128,144,160,176},{192,208,224,240},{256,27..., dimensions={0} | all-to-all | bytes 1081344 | tf_op jit(solution)/shard_map/all_to_all | solution.py:352
  91.9 1.9 %collective-permute-start.9 = (f32[232,512]{1,0:T(8,128)S(1)}, f32[232,512]{1,0:T(8,128)S(1)}, u32[]{:S(2)}, u32[]{:S(2)}) collective-permute-start(f32[232,512]{1,0:T(8,128)S(1)} %get-tuple-element.28), channel_id=1, source_target_pairs={{0,72},{8,64},{64,8},{72,0},{16,88},{24,80},{80,24},{88,16},{32,10... | collective-permute-start | bytes 1425416 | tf_op jit(solution)/shard_map/ppermute | solution.py:388
  93.8 4.6 %collective-permute-start.6 = (f32[232,512]{1,0:T(8,128)S(1)}, f32[232,512]{1,0:T(8,128)S(1)}, u32[]{:S(2)}, u32[]{:S(2)}) collective-permute-start(f32[232,512]{1,0:T(8,128)S(1)} %get-tuple-element.25), channel_id=1, source_target_pairs={{0,64},{8,72},{64,0},{72,8},{16,80},{24,88},{80,16},{88,24},{32,96... | collective-permute-start | bytes 1425416 | tf_op jit(solution)/shard_map/ppermute | solution.py:388
  98.4 4.3 %collective-permute-start.7 = (f32[232,512]{1,0:T(8,128)S(1)}, f32[232,512]{1,0:T(8,128)S(1)}, u32[]{:S(2)}, u32[]{:S(2)}) collective-permute-start(f32[232,512]{1,0:T(8,128)S(1)} %get-tuple-element.26), channel_id=1, source_target_pairs={{0,8},{8,0},{64,72},{72,64},{16,24},{24,16},{80,88},{88,80},{32,40... | collective-permute-start | bytes 1425416 | tf_op jit(solution)/shard_map/ppermute | solution.py:388
  102.7 2.0 %collective-permute-done.9.refs_1_ = f32[232,512]{1,0:T(8,128)S(1)} collective-permute-done((f32[232,512]{1,0:T(8,128)S(1)}, f32[232,512]{1,0:T(8,128)S(1)}, u32[]{:S(2)}, u32[]{:S(2)}) %collective-permute-start.9) | collective-permute-done | bytes 475168 | tf_op jit(solution)/shard_map/ppermute | solution.py:388
  105.1 4.1 %collective-permute-start.10 = (f32[2,128,512]{2,1,0:T(8,128)S(1)}, f32[2,128,512]{2,1,0:T(8,128)S(1)}, u32[]{:S(2)}, u32[]{:S(2)}) collective-permute-start(f32[2,128,512]{2,1,0:T(8,128)S(1)} %shard_map.69), channel_id=1, source_target_pairs={{0,4},{4,0},{8,12},{12,8},{16,20},{20,16},{24,28},{28,24},{32,36},... | collective-permute-start | bytes 1572872 | tf_op jit(solution)/shard_map/ppermute | solution.py:456
  109.2 0.4 collective-permute-done.7.refs_1_
  110.1 4.9 %collective-permute-start.8 = (f32[2,128,512]{2,1,0:T(8,128)S(1)}, f32[2,128,512]{2,1,0:T(8,128)S(1)}, u32[]{:S(2)}, u32[]{:S(2)}) collective-permute-start(f32[2,128,512]{2,1,0:T(8,128)S(1)} %shard_map.68), channel_id=1, source_target_pairs={{0,4},{4,0},{8,12},{12,8},{16,20},{20,16},{24,28},{28,24},{32,36},... | collective-permute-start | bytes 1572872 | tf_op jit(solution)/shard_map/ppermute | solution.py:459
  115.0 1.2 shard_map.70.refs_3_
  116.2 1.2 %shard_map.71.filled_ref = f32[128,4096]{1,0:T(8,128)} custom-call(s32[1]{0:T(128)S(6)} %copy.18.level_ref, f32[8,128]{1,0:T(8,128)S(1)} %shard_map.58.meta_ref, bf16[9,128,232]{2,1,0:T(8,128)(2,1)S(1)} %copy-done.2, f32[232,512]{1,0:T(8,128)S(1)} %collective-permute-done.6.refs_0_, ...), custom_call_target="tpu_custom_call", output_to_operand_aliasing={{}: (6, {})} | custom-call | flops 1000000000 | tf_op jit(solution)/shard_map/pallas_call | solution.py:443
  117.4 0.8 shard_map.72
  (25 shorter events, 2.3 us)
Async XLA Ops:
  0.0 1.8 %copy-start.1 = (f32[1,128,4096]{2,1,0:T(8,128)S(1)}, f32[1,128,4096]{2,1,0:T(8,128)}, u32[]{:S(2)}) copy-start(f32[1,128,4096]{2,1,0:T(8,128)} %param.6) | copy-start | bytes 6291460
  0.0 20.4 %copy-start = (bf16[9,240,272]{2,1,0:T(8,128)(2,1)S(1)}, bf16[9,240,272]{2,1,0:T(8,128)(2,1)}, u32[]{:S(2)}) copy-start(bf16[9,240,272]{2,1,0:T(8,128)(2,1)} %constant.4.clone.table_ref) | copy-start | bytes 3525124
  1.9 18.5 %collective-permute-start = (f32[136,2048]{1,0:T(8,128)S(1)}, f32[136,2048]{1,0:T(8,128)S(1)}, u32[]{:S(2)}, u32[]{:S(2)}) collective-permute-start(f32[136,2048]{1,0:T(8,128)S(1)} %get-tuple-element.17), channel_id=1, source_target_pairs={{0,4},{4,0},{8,12},{12,8},{16,20},{20,16},{24,28},{28,24},{32,36},... | collective-permute-start | bytes 3342344 | tf_op jit(solution)/shard_map/ppermute | solution.py:409
  10.7 6.9 %collective-permute-start.1 = (f32[8,4096]{1,0:T(8,128)S(1)}, f32[8,4096]{1,0:T(8,128)S(1)}, u32[]{:S(2)}, u32[]{:S(2)}) collective-permute-start(f32[8,4096]{1,0:T(8,128)S(1)} %get-tuple-element.18), channel_id=1, source_target_pairs={{0,3},{1,0},{2,1},{3,2},{4,7},{5,4},{6,5},{7,6},{8,11},{9,8},{10,9... | collective-permute-start | bytes 393224 | tf_op jit(solution)/shard_map/ppermute | solution.py:408
  17.6 3.7 %collective-permute-start.2 = (f32[8,2048]{1,0:T(8,128)S(1)}, f32[8,2048]{1,0:T(8,128)S(1)}, u32[]{:S(2)}, u32[]{:S(2)}) collective-permute-start(f32[8,2048]{1,0:T(8,128)S(1)} %shard_map.59), channel_id=1, source_target_pairs={{0,4},{4,0},{8,12},{12,8},{16,20},{20,16},{24,28},{28,24},{32,36},... | collective-permute-start | bytes 196616 | tf_op jit(solution)/shard_map/ppermute | solution.py:411
  21.9 13.4 %collective-permute-start.3 = (f32[240,512]{1,0:T(8,128)S(1)}, f32[240,512]{1,0:T(8,128)S(1)}, u32[]{:S(2)}, u32[]{:S(2)}) collective-permute-start(f32[240,512]{1,0:T(8,128)S(1)} %get-tuple-element.22), channel_id=1, source_target_pairs={{0,8},{8,0},{64,72},{72,64},{16,24},{24,16},{80,88},{88,80},{32,40... | collective-permute-start | bytes 1474568 | tf_op jit(solution)/shard_map/ppermute | solution.py:388
  27.5 11.4 %collective-permute-start.4 = (f32[240,512]{1,0:T(8,128)S(1)}, f32[240,512]{1,0:T(8,128)S(1)}, u32[]{:S(2)}, u32[]{:S(2)}) collective-permute-start(f32[240,512]{1,0:T(8,128)S(1)} %get-tuple-element.23), channel_id=1, source_target_pairs={{0,64},{8,72},{64,0},{72,8},{16,80},{24,88},{80,16},{88,24},{32,96... | collective-permute-start | bytes 1474568 | tf_op jit(solution)/shard_map/ppermute | solution.py:388
  32.6 12.9 %collective-permute-start.5 = (f32[240,512]{1,0:T(8,128)S(1)}, f32[240,512]{1,0:T(8,128)S(1)}, u32[]{:S(2)}, u32[]{:S(2)}) collective-permute-start(f32[240,512]{1,0:T(8,128)S(1)} %get-tuple-element.24), channel_id=1, source_target_pairs={{0,72},{8,64},{64,8},{72,0},{16,88},{24,80},{80,24},{88,16},{32,10... | collective-permute-start | bytes 1474568 | tf_op jit(solution)/shard_map/ppermute | solution.py:388
  77.1 27.5 %copy-start.2 = (bf16[9,128,232]{2,1,0:T(8,128)(2,1)S(1)}, bf16[9,128,232]{2,1,0:T(8,128)(2,1)}, u32[]{:S(2)}) copy-start(bf16[9,128,232]{2,1,0:T(8,128)(2,1)} %constant.5.clone.table_ref) | copy-start | bytes 1603588
  91.9 12.8 %collective-permute-start.9 = (f32[232,512]{1,0:T(8,128)S(1)}, f32[232,512]{1,0:T(8,128)S(1)}, u32[]{:S(2)}, u32[]{:S(2)}) collective-permute-start(f32[232,512]{1,0:T(8,128)S(1)} %get-tuple-element.28), channel_id=1, source_target_pairs={{0,72},{8,64},{64,8},{72,0},{16,88},{24,80},{80,24},{88,16},{32,10... | collective-permute-start | bytes 1425416 | tf_op jit(solution)/shard_map/ppermute | solution.py:388
  93.8 15.4 %collective-permute-start.6 = (f32[232,512]{1,0:T(8,128)S(1)}, f32[232,512]{1,0:T(8,128)S(1)}, u32[]{:S(2)}, u32[]{:S(2)}) collective-permute-start(f32[232,512]{1,0:T(8,128)S(1)} %get-tuple-element.25), channel_id=1, source_target_pairs={{0,64},{8,72},{64,0},{72,8},{16,80},{24,88},{80,16},{88,24},{32,96... | collective-permute-start | bytes 1425416 | tf_op jit(solution)/shard_map/ppermute | solution.py:388
  98.4 11.3 %collective-permute-start.7 = (f32[232,512]{1,0:T(8,128)S(1)}, f32[232,512]{1,0:T(8,128)S(1)}, u32[]{:S(2)}, u32[]{:S(2)}) collective-permute-start(f32[232,512]{1,0:T(8,128)S(1)} %get-tuple-element.26), channel_id=1, source_target_pairs={{0,8},{8,0},{64,72},{72,64},{16,24},{24,16},{80,88},{88,80},{32,40... | collective-permute-start | bytes 1425416 | tf_op jit(solution)/shard_map/ppermute | solution.py:388
  105.1 11.1 %collective-permute-start.10 = (f32[2,128,512]{2,1,0:T(8,128)S(1)}, f32[2,128,512]{2,1,0:T(8,128)S(1)}, u32[]{:S(2)}, u32[]{:S(2)}) collective-permute-start(f32[2,128,512]{2,1,0:T(8,128)S(1)} %shard_map.69), channel_id=1, source_target_pairs={{0,4},{4,0},{8,12},{12,8},{16,20},{20,16},{24,28},{28,24},{32,36},... | collective-permute-start | bytes 1572872 | tf_op jit(solution)/shard_map/ppermute | solution.py:456
  110.1 7.4 %collective-permute-start.8 = (f32[2,128,512]{2,1,0:T(8,128)S(1)}, f32[2,128,512]{2,1,0:T(8,128)S(1)}, u32[]{:S(2)}, u32[]{:S(2)}) collective-permute-start(f32[2,128,512]{2,1,0:T(8,128)S(1)} %shard_map.68), channel_id=1, source_target_pairs={{0,4},{4,0},{8,12},{12,8},{16,20},{20,16},{24,28},{28,24},{32,36},... | collective-permute-start | bytes 1572872 | tf_op jit(solution)/shard_map/ppermute | solution.py:459

commit v6 on v5

--- a/solution.py
+++ b/solution.py
@@ -292,11 +292,11 @@
             i += 1
 
 
-def other_copies(turns, values_ref, out_ref, sems):
-    first = (1 - core_here()) * (out_ref.shape[1] // 2)
+def piece_copies(turns, core, flip, values_ref, out_ref, sems):
+    first = core * (out_ref.shape[1] // 2)
     width = values_ref.shape[2]
     for i, turn in enumerate(turns):
-        start = pl.multiple_of(first + (piece_here(turn) ^ 3) * width, LANES)
+        start = pl.multiple_of(first + (piece_here(turn) ^ flip) * width, LANES)
         yield pltpu.make_async_copy(values_ref.at[i], out_ref.at[:, pl.ds(start, width)], sems.at[i])
 
 
@@ -315,17 +315,22 @@
     run(own_copies(turns, levels_in(level_ref, meta_ref), table_ref, got_refs, out_ref, done_ref, sems))
 
 
-def late_kernel(turns, placed, level_ref, meta_ref, table_ref, *refs):
-    *got_refs, values_ref, filled_ref, out_ref, done_ref, sems, other_sems = refs
-    levels = levels_in(level_ref, meta_ref)
+def late_kernel(level_ref, meta_ref, table_ref, *refs):
+    *got_refs, out_ref = refs
+    own, other = levels_in(level_ref, meta_ref)
+    table = table_ref[own * 3 + other]
+    for i, ref in enumerate(got_refs):
+        for low, values in pieces(ref):
+            out_ref[i, :, low : low + values.shape[1]] = two_part_dot(table, values)
+
+
+def place_kernel(early, late, early_ref, own_ref, late_ref, filled_ref, out_ref, sems):
+    core = core_here()
     run(
-        other_copies(placed, values_ref, out_ref, other_sems),
-        own_copies(turns, levels, table_ref, got_refs, out_ref, done_ref, sems),
+        piece_copies(early, 1 - core, 3, early_ref, out_ref, sems.at[0]),
+        piece_copies(late, core, 0, own_ref, out_ref, sems.at[1]),
+        piece_copies(late, 1 - core, 3, late_ref, out_ref, sems.at[2]),
     )
-
-
-def place_kernel(turns, values_ref, filled_ref, out_ref, sems):
-    run(other_copies(turns, values_ref, out_ref, sems))
 
 
 def member(y, z, core):
@@ -439,26 +444,19 @@
             parts, flops=10**9,
         )(first_level, meta, back, *[final[turn] for turn in turns])
 
-    def own_late_rows(turns, placed, values, filled):
-        return call(
-            functools.partial(late_kernel, turns, placed), [SMEM] + [VMEM] * 5 + [HBM], HBM,
-            f32(ROWS, width), (*parts, DMA((2,))), flops=10**9, alias={6: 0},
-        )(first_level, meta, back, *[final[turn] for turn in turns], values, filled)
-
-    def place(turns, values, filled):
-        return call(
-            functools.partial(place_kernel, turns), [VMEM, HBM], HBM, f32(ROWS, width),
-            (DMA((2,)),), alias={1: 0}, flops=10**8,
-        )(values, filled)
-
     early, late = (0, 3), (2, 1)
     other_early = other_rows(early)
     swapped_early = lax.ppermute(other_early, "grp", swap)
     out = own_early_rows(early)
     other_late = other_rows(late)
     swapped_late = lax.ppermute(other_late, "grp", swap)
-    out = own_late_rows(late, early, swapped_early, out)
-    out = place(late, swapped_late, out)
+    own_late = call(
+        late_kernel, [SMEM] + [VMEM] * 4, VMEM, f32(len(late), ROWS, chunk), flops=10**9
+    )(first_level, meta, back, *[final[turn] for turn in late])
+    out = call(
+        functools.partial(place_kernel, early, late), [VMEM] * 3 + [HBM], HBM, f32(ROWS, width),
+        (DMA((3, 2)),), alias={3: 0}, flops=10**8,
+    )(swapped_early, own_late, swapped_late, out)
     return out[None]
 
 

time: 119 us -> 118 us (level)
  transfers between devices with their start and end apart: 11 -> 11, of which waited for: 6 -> 6; matrix products, arithmetic and copies ran while one was open for 0% -> 0% of each run, Pallas kernels for 4% -> 3%
where the time goes in v6:
time: 118 us
  starting transfers between devices  45.9 us (39%)
  blocking collectives  45.9 us (39%)
  waiting for transfers between devices  17.8 us (15%)
  Pallas kernels  6.2 us (5%)
  between operations  2.05 us (2%)
    all_to_all x3, blocking collectives, exchange(): lax.all_to_all(values, 'grp', 0, 0, axis_index_groups=groups, tiled=True)  45.9 us
    ppermute x6, starting transfers between devices, through_tile(): far[turn] = lax.ppermute(pieces[turn], 'grp', turned(turn))  23.4 us
    ppermute x6, waiting for transfers between devices, through_tile(): far[turn] = lax.ppermute(pieces[turn], 'grp', turned(turn))  12.6 us
    ppermute x1, starting transfers between devices, shards(): other = lax.ppermute(entry, 'grp', swap)  8.75 us
    ppermute x1, waiting for transfers between devices, shards(): next_plane = lax.ppermute(plane, 'slab', to_previous)  5.01 us
    ppermute x1, starting transfers between devices, shards(): swapped_late = lax.ppermute(other_late, 'grp', swap)  4.93 us
    ppermute x1, starting transfers between devices, shards(): swapped_early = lax.ppermute(other_early, 'grp', swap)  4.14 us
    ppermute x1, starting transfers between devices, shards(): other_next = lax.ppermute(cut, 'grp', swap)  2.77 us
  transfers between devices with their start and end apart: 11, of which 6 were waited for; matrix products, arithmetic and copies ran while one was open for 0% of the time, Pallas kernels for 3%

profile of v6, /device:TPU:1, one launch (start us, length us, event | category | flops | bytes accessed | tf_op | source)
XLA Modules:
  0.0 117.9 jit_solution(17226663379435493473)
XLA Ops:
  1.9 8.7 %collective-permute-start = (f32[136,2048]{1,0:T(8,128)S(1)}, f32[136,2048]{1,0:T(8,128)S(1)}, u32[]{:S(2)}, u32[]{:S(2)}) collective-permute-start(f32[136,2048]{1,0:T(8,128)S(1)} %get-tuple-element.17), channel_id=1, source_target_pairs={{0,4},{4,0},{8,12},{12,8},{16,20},{20,16},{24,28},{28,24},{32,36},... | collective-permute-start | bytes 3342344 | tf_op jit(solution)/shard_map/ppermute | solution.py:414
  10.7 1.9 %collective-permute-start.1 = (f32[8,4096]{1,0:T(8,128)S(1)}, f32[8,4096]{1,0:T(8,128)S(1)}, u32[]{:S(2)}, u32[]{:S(2)}) collective-permute-start(f32[8,4096]{1,0:T(8,128)S(1)} %get-tuple-element.18), channel_id=1, source_target_pairs={{0,3},{1,0},{2,1},{3,2},{4,7},{5,4},{6,5},{7,6},{8,11},{9,8},{10,9... | collective-permute-start | bytes 393224 | tf_op jit(solution)/shard_map/ppermute | solution.py:413
  12.6 5.0 %collective-permute-done.1.plane_ref = f32[8,4096]{1,0:T(8,128)S(1)} collective-permute-done((f32[8,4096]{1,0:T(8,128)S(1)}, f32[8,4096]{1,0:T(8,128)S(1)}, u32[]{:S(2)}, u32[]{:S(2)}) %collective-permute-start.1) | collective-permute-done | bytes 131104 | tf_op jit(solution)/shard_map/ppermute | solution.py:413
  17.6 2.8 %collective-permute-start.2 = (f32[8,2048]{1,0:T(8,128)S(1)}, f32[8,2048]{1,0:T(8,128)S(1)}, u32[]{:S(2)}, u32[]{:S(2)}) collective-permute-start(f32[8,2048]{1,0:T(8,128)S(1)} %shard_map.59), channel_id=1, source_target_pairs={{0,4},{4,0},{8,12},{12,8},{16,20},{20,16},{24,28},{28,24},{32,36},... | collective-permute-start | bytes 196616 | tf_op jit(solution)/shard_map/ppermute | solution.py:416
  20.4 0.7 shard_map.62
  21.3 0.6 shard_map.63
  21.9 5.6 %collective-permute-start.3 = (f32[240,512]{1,0:T(8,128)S(1)}, f32[240,512]{1,0:T(8,128)S(1)}, u32[]{:S(2)}, u32[]{:S(2)}) collective-permute-start(f32[240,512]{1,0:T(8,128)S(1)} %get-tuple-element.22), channel_id=1, source_target_pairs={{0,8},{8,0},{64,72},{72,64},{16,24},{24,16},{80,88},{88,80},{32,40... | collective-permute-start | bytes 1474568 | tf_op jit(solution)/shard_map/ppermute | solution.py:393
  27.5 5.1 %collective-permute-start.4 = (f32[240,512]{1,0:T(8,128)S(1)}, f32[240,512]{1,0:T(8,128)S(1)}, u32[]{:S(2)}, u32[]{:S(2)}) collective-permute-start(f32[240,512]{1,0:T(8,128)S(1)} %get-tuple-element.23), channel_id=1, source_target_pairs={{0,64},{8,72},{64,0},{72,8},{16,80},{24,88},{80,16},{88,24},{32,96... | collective-permute-start | bytes 1474568 | tf_op jit(solution)/shard_map/ppermute | solution.py:393
  32.6 1.9 %collective-permute-start.5 = (f32[240,512]{1,0:T(8,128)S(1)}, f32[240,512]{1,0:T(8,128)S(1)}, u32[]{:S(2)}, u32[]{:S(2)}) collective-permute-start(f32[240,512]{1,0:T(8,128)S(1)} %get-tuple-element.24), channel_id=1, source_target_pairs={{0,72},{8,64},{64,8},{72,0},{16,88},{24,80},{80,24},{88,16},{32,10... | collective-permute-start | bytes 1474568 | tf_op jit(solution)/shard_map/ppermute | solution.py:393
  35.3 3.6 %collective-permute-done.4.refs_2_ = f32[240,512]{1,0:T(8,128)S(1)} collective-permute-done((f32[240,512]{1,0:T(8,128)S(1)}, f32[240,512]{1,0:T(8,128)S(1)}, u32[]{:S(2)}, u32[]{:S(2)}) %collective-permute-start.4) | collective-permute-done | bytes 491552 | tf_op jit(solution)/shard_map/ppermute | solution.py:393
  39.0 6.6 %collective-permute-done.5.refs_3_ = f32[240,512]{1,0:T(8,128)S(1)} collective-permute-done((f32[240,512]{1,0:T(8,128)S(1)}, f32[240,512]{1,0:T(8,128)S(1)}, u32[]{:S(2)}, u32[]{:S(2)}) %collective-permute-start.5) | collective-permute-done | bytes 491552 | tf_op jit(solution)/shard_map/ppermute | solution.py:393
  45.7 15.2 %all_to_all.15.got_ref = f32[4,264,128]{2,1,0:T(8,128)S(1)} all-to-all(f32[4,264,128]{2,1,0:T(8,128)S(1)} %shard_map.64), channel_id=1, replica_groups={{0,16,32,48},{64,80,96,112},{128,144,160,176},{192,208,224,240},{256,27..., dimensions={0} | all-to-all | bytes 1081344 | tf_op jit(solution)/shard_map/all_to_all | solution.py:357
  61.0 16.1 %all_to_all.16.got_ref = f32[4,264,128]{2,1,0:T(8,128)S(1)} all-to-all(f32[4,264,128]{2,1,0:T(8,128)S(1)} %shard_map.65), channel_id=1, replica_groups={{0,128,256,384},{8,136,264,392},{16,144,272,400},{24,152,280,408},{32,1..., dimensions={0} | all-to-all | bytes 1081344 | tf_op jit(solution)/shard_map/all_to_all | solution.py:357
  77.2 14.5 %all_to_all.17.table_ref = f32[4,264,128]{2,1,0:T(8,128)S(1)} all-to-all(f32[4,264,128]{2,1,0:T(8,128)S(1)} %shard_map.66), channel_id=1, replica_groups={{0,16,32,48},{64,80,96,112},{128,144,160,176},{192,208,224,240},{256,27..., dimensions={0} | all-to-all | bytes 1081344 | tf_op jit(solution)/shard_map/all_to_all | solution.py:357
  91.9 1.9 %collective-permute-start.6 = (f32[232,512]{1,0:T(8,128)S(1)}, f32[232,512]{1,0:T(8,128)S(1)}, u32[]{:S(2)}, u32[]{:S(2)}) collective-permute-start(f32[232,512]{1,0:T(8,128)S(1)} %get-tuple-element.26), channel_id=1, source_target_pairs={{0,72},{8,64},{64,8},{72,0},{16,88},{24,80},{80,24},{88,16},{32,10... | collective-permute-start | bytes 1425416 | tf_op jit(solution)/shard_map/ppermute | solution.py:393
  93.8 4.6 %collective-permute-start.8 = (f32[232,512]{1,0:T(8,128)S(1)}, f32[232,512]{1,0:T(8,128)S(1)}, u32[]{:S(2)}, u32[]{:S(2)}) collective-permute-start(f32[232,512]{1,0:T(8,128)S(1)} %get-tuple-element.27), channel_id=1, source_target_pairs={{0,64},{8,72},{64,0},{72,8},{16,80},{24,88},{80,16},{88,24},{32,96... | collective-permute-start | bytes 1425416 | tf_op jit(solution)/shard_map/ppermute | solution.py:393
  98.4 4.3 %collective-permute-start.9 = (f32[232,512]{1,0:T(8,128)S(1)}, f32[232,512]{1,0:T(8,128)S(1)}, u32[]{:S(2)}, u32[]{:S(2)}) collective-permute-start(f32[232,512]{1,0:T(8,128)S(1)} %get-tuple-element.28), channel_id=1, source_target_pairs={{0,8},{8,0},{64,72},{72,64},{16,24},{24,16},{80,88},{88,80},{32,40... | collective-permute-start | bytes 1425416 | tf_op jit(solution)/shard_map/ppermute | solution.py:393
  102.7 2.0 %collective-permute-done.6.refs_1_ = f32[232,512]{1,0:T(8,128)S(1)} collective-permute-done((f32[232,512]{1,0:T(8,128)S(1)}, f32[232,512]{1,0:T(8,128)S(1)}, u32[]{:S(2)}, u32[]{:S(2)}) %collective-permute-start.6) | collective-permute-done | bytes 475168 | tf_op jit(solution)/shard_map/ppermute | solution.py:393
  105.1 4.1 %collective-permute-start.7 = (f32[2,128,512]{2,1,0:T(8,128)S(1)}, f32[2,128,512]{2,1,0:T(8,128)S(1)}, u32[]{:S(2)}, u32[]{:S(2)}) collective-permute-start(f32[2,128,512]{2,1,0:T(8,128)S(1)} %shard_map.68), channel_id=1, source_target_pairs={{0,4},{4,0},{8,12},{12,8},{16,20},{20,16},{24,28},{28,24},{32,36},... | collective-permute-start | bytes 1572872 | tf_op jit(solution)/shard_map/ppermute | solution.py:449
  109.3 0.4 collective-permute-done.9.refs_1_
  109.7 0.4 shard_map.70
  110.1 4.9 %collective-permute-start.10 = (f32[2,128,512]{2,1,0:T(8,128)S(1)}, f32[2,128,512]{2,1,0:T(8,128)S(1)}, u32[]{:S(2)}, u32[]{:S(2)}) collective-permute-start(f32[2,128,512]{2,1,0:T(8,128)S(1)} %shard_map.70), channel_id=1, source_target_pairs={{0,4},{4,0},{8,12},{12,8},{16,20},{20,16},{24,28},{28,24},{32,36},... | collective-permute-start | bytes 1572872 | tf_op jit(solution)/shard_map/ppermute | solution.py:452
  115.5 1.2 shard_map.71.filled_ref
  116.6 1.2 %shard_map.72 = f32[128,4096]{1,0:T(8,128)} custom-call(f32[2,128,512]{2,1,0:T(8,128)S(1)} %collective-permute-done.7.early_ref, f32[2,128,512]{2,1,0:T(8,128)S(1)} %shard_map.69.own_ref, f32[2,128,512]{2,1,0:T(8,128)S(1)} %collective-permute-done.10.late_ref, f32[128,4096]{1,0:T(8,128)} %shard_map.71.filled_ref), custom_call_target="tpu_custom_call", output_to_operand_aliasing={{}: (3, {})} | custom-call | flops 100000000 | tf_op jit(solution)/shard_map/pallas_call | solution.py:456
  (25 shorter events, 2.4 us)
Async XLA Ops:
  0.0 1.8 %copy-start.1 = (f32[1,128,4096]{2,1,0:T(8,128)S(1)}, f32[1,128,4096]{2,1,0:T(8,128)}, u32[]{:S(2)}) copy-start(f32[1,128,4096]{2,1,0:T(8,128)} %param.6) | copy-start | bytes 6291460
  0.0 20.4 %copy-start = (bf16[9,240,272]{2,1,0:T(8,128)(2,1)S(1)}, bf16[9,240,272]{2,1,0:T(8,128)(2,1)}, u32[]{:S(2)}) copy-start(bf16[9,240,272]{2,1,0:T(8,128)(2,1)} %constant.4.clone.table_ref) | copy-start | bytes 3525124
  1.9 18.5 %collective-permute-start = (f32[136,2048]{1,0:T(8,128)S(1)}, f32[136,2048]{1,0:T(8,128)S(1)}, u32[]{:S(2)}, u32[]{:S(2)}) collective-permute-start(f32[136,2048]{1,0:T(8,128)S(1)} %get-tuple-element.17), channel_id=1, source_target_pairs={{0,4},{4,0},{8,12},{12,8},{16,20},{20,16},{24,28},{28,24},{32,36},... | collective-permute-start | bytes 3342344 | tf_op jit(solution)/shard_map/ppermute | solution.py:414
  10.7 6.9 %collective-permute-start.1 = (f32[8,4096]{1,0:T(8,128)S(1)}, f32[8,4096]{1,0:T(8,128)S(1)}, u32[]{:S(2)}, u32[]{:S(2)}) collective-permute-start(f32[8,4096]{1,0:T(8,128)S(1)} %get-tuple-element.18), channel_id=1, source_target_pairs={{0,3},{1,0},{2,1},{3,2},{4,7},{5,4},{6,5},{7,6},{8,11},{9,8},{10,9... | collective-permute-start | bytes 393224 | tf_op jit(solution)/shard_map/ppermute | solution.py:413
  17.6 3.7 %collective-permute-start.2 = (f32[8,2048]{1,0:T(8,128)S(1)}, f32[8,2048]{1,0:T(8,128)S(1)}, u32[]{:S(2)}, u32[]{:S(2)}) collective-permute-start(f32[8,2048]{1,0:T(8,128)S(1)} %shard_map.59), channel_id=1, source_target_pairs={{0,4},{4,0},{8,12},{12,8},{16,20},{20,16},{24,28},{28,24},{32,36},... | collective-permute-start | bytes 196616 | tf_op jit(solution)/shard_map/ppermute | solution.py:416
  21.9 13.4 %collective-permute-start.3 = (f32[240,512]{1,0:T(8,128)S(1)}, f32[240,512]{1,0:T(8,128)S(1)}, u32[]{:S(2)}, u32[]{:S(2)}) collective-permute-start(f32[240,512]{1,0:T(8,128)S(1)} %get-tuple-element.22), channel_id=1, source_target_pairs={{0,8},{8,0},{64,72},{72,64},{16,24},{24,16},{80,88},{88,80},{32,40... | collective-permute-start | bytes 1474568 | tf_op jit(solution)/shard_map/ppermute | solution.py:393
  27.5 11.4 %collective-permute-start.4 = (f32[240,512]{1,0:T(8,128)S(1)}, f32[240,512]{1,0:T(8,128)S(1)}, u32[]{:S(2)}, u32[]{:S(2)}) collective-permute-start(f32[240,512]{1,0:T(8,128)S(1)} %get-tuple-element.23), channel_id=1, source_target_pairs={{0,64},{8,72},{64,0},{72,8},{16,80},{24,88},{80,16},{88,24},{32,96... | collective-permute-start | bytes 1474568 | tf_op jit(solution)/shard_map/ppermute | solution.py:393
  32.6 12.9 %collective-permute-start.5 = (f32[240,512]{1,0:T(8,128)S(1)}, f32[240,512]{1,0:T(8,128)S(1)}, u32[]{:S(2)}, u32[]{:S(2)}) collective-permute-start(f32[240,512]{1,0:T(8,128)S(1)} %get-tuple-element.24), channel_id=1, source_target_pairs={{0,72},{8,64},{64,8},{72,0},{16,88},{24,80},{80,24},{88,16},{32,10... | collective-permute-start | bytes 1474568 | tf_op jit(solution)/shard_map/ppermute | solution.py:393
  77.1 27.6 %copy-start.2 = (bf16[9,128,232]{2,1,0:T(8,128)(2,1)S(1)}, bf16[9,128,232]{2,1,0:T(8,128)(2,1)}, u32[]{:S(2)}) copy-start(bf16[9,128,232]{2,1,0:T(8,128)(2,1)} %constant.5.clone.table_ref) | copy-start | bytes 1603588
  91.9 12.8 %collective-permute-start.6 = (f32[232,512]{1,0:T(8,128)S(1)}, f32[232,512]{1,0:T(8,128)S(1)}, u32[]{:S(2)}, u32[]{:S(2)}) collective-permute-start(f32[232,512]{1,0:T(8,128)S(1)} %get-tuple-element.26), channel_id=1, source_target_pairs={{0,72},{8,64},{64,8},{72,0},{16,88},{24,80},{80,24},{88,16},{32,10... | collective-permute-start | bytes 1425416 | tf_op jit(solution)/shard_map/ppermute | solution.py:393
  93.8 15.4 %collective-permute-start.8 = (f32[232,512]{1,0:T(8,128)S(1)}, f32[232,512]{1,0:T(8,128)S(1)}, u32[]{:S(2)}, u32[]{:S(2)}) collective-permute-start(f32[232,512]{1,0:T(8,128)S(1)} %get-tuple-element.27), channel_id=1, source_target_pairs={{0,64},{8,72},{64,0},{72,8},{16,80},{24,88},{80,16},{88,24},{32,96... | collective-permute-start | bytes 1425416 | tf_op jit(solution)/shard_map/ppermute | solution.py:393
  98.4 11.3 %collective-permute-start.9 = (f32[232,512]{1,0:T(8,128)S(1)}, f32[232,512]{1,0:T(8,128)S(1)}, u32[]{:S(2)}, u32[]{:S(2)}) collective-permute-start(f32[232,512]{1,0:T(8,128)S(1)} %get-tuple-element.28), channel_id=1, source_target_pairs={{0,8},{8,0},{64,72},{72,64},{16,24},{24,16},{80,88},{88,80},{32,40... | collective-permute-start | bytes 1425416 | tf_op jit(solution)/shard_map/ppermute | solution.py:393
  105.1 11.5 %collective-permute-start.7 = (f32[2,128,512]{2,1,0:T(8,128)S(1)}, f32[2,128,512]{2,1,0:T(8,128)S(1)}, u32[]{:S(2)}, u32[]{:S(2)}) collective-permute-start(f32[2,128,512]{2,1,0:T(8,128)S(1)} %shard_map.68), channel_id=1, source_target_pairs={{0,4},{4,0},{8,12},{12,8},{16,20},{20,16},{24,28},{28,24},{32,36},... | collective-permute-start | bytes 1572872 | tf_op jit(solution)/shard_map/ppermute | solution.py:449
  110.1 6.5 %collective-permute-start.10 = (f32[2,128,512]{2,1,0:T(8,128)S(1)}, f32[2,128,512]{2,1,0:T(8,128)S(1)}, u32[]{:S(2)}, u32[]{:S(2)}) collective-permute-start(f32[2,128,512]{2,1,0:T(8,128)S(1)} %shard_map.70), channel_id=1, source_target_pairs={{0,4},{4,0},{8,12},{12,8},{16,20},{20,16},{24,28},{28,24},{32,36},... | collective-permute-start | bytes 1572872 | tf_op jit(solution)/shard_map/ppermute | solution.py:452
